TPU v7x, 32 devices: a whole 2x2x4 slice. The times are simulated.
32 devices in a mesh: gx: 8 (over z, x), gy: 4 (over y, core).
Axes of the slice: x: 2, y: 2, z: 4, core: 2. Of those that a mesh axis runs over, the one named last changes fastest.
Arguments:
- base_state: float32 [4, 8, 512, 512], P(None, None, 'gx', 'gy'), may hold values from -6 to 6
- base_old: float32 [4, 8, 512, 512], P(None, None, 'gx', 'gy'), may hold values from -6 to 6
- fine_state: float32 [4, 8, 8, 264, 264], P(None, None, 'gx', 'gy'), may hold values from -6 to 6
- fine_old: float32 [4, 8, 8, 264, 264], P(None, None, 'gx', 'gy'), may hold values from -6 to 6
- coupling: float32 [4, 4], replicated, may hold values from -12 to 12
- patch_offsets: int32 [8, 2], replicated, may hold values from 1 to 423, as said below
- patch_group: int32 [8], replicated, may hold values from 0 to 7, each once
Outputs:
- base_residual: float32 [4, 8, 512, 512], P(None, None, 'gx', 'gy')
- fine_residual: float32 [4, 8, 8, 264, 264], P(None, None, 'gx', 'gy')
- residual_norm: float32 [], replicated
Inputs may be any that keep to these rules, and one draw needn't show every extreme that they name: `patch_offsets`: with the cycle of one base cell around it, each patch lies inside the grid, and no two patches or cycles share a cell. `patch_group`: every group owns exactly one patch.
All inputs are finite; a program needn't handle non-finite values.
Results may differ from a plain program's by a relative error of at most 0.0003.
Values sent between devices are 32-bit elements; how exact they have to be, the bound alone decides.
A program may use at most 128 MiB of HBM per device.

v0:
```python
import jax
import jax.numpy as jnp
from jax import lax
from jax.sharding import PartitionSpec as P

PC = 88
RATIO = 3


time_step = 0.1
viscosity = 0.2
vertical_mix = 0.5


def padded_2(block, sides, width):
    for axis, dim in sides:
        count = lax.axis_size(axis)
        forward = [(i, i + 1) for i in range(count - 1)]
        backward = [(target, source) for source, target in forward]
        low = lax.ppermute(
            lax.slice_in_dim(block, block.shape[dim] - width, None, axis=dim), axis, forward
        )
        high = lax.ppermute(lax.slice_in_dim(block, 0, width, axis=dim), axis, backward)
        block = jnp.concatenate([low, block, high], axis=dim)
    return block


def tendency(padded, state, former, coupling, inverse):
    north = padded[:, :, 2:, 1:-1]
    south = padded[:, :, :-2, 1:-1]
    east = padded[:, :, 1:-1, 2:]
    west = padded[:, :, 1:-1, :-2]
    advect = (state[0:1] * (north - south) + state[1:2] * (east - west)) * (0.5 * inverse)
    laplace = (north + south + east + west - 4.0 * state) * (inverse * inverse)
    zero_level = jnp.zeros_like(state[:, :1])
    upper = jnp.concatenate([state[:, 1:], zero_level], axis=1)
    lower = jnp.concatenate([zero_level, state[:, :-1]], axis=1)
    vertical = 2.0 * state - upper - lower
    coupled = coupling[:, 0, None, None, None] * state[0:1]
    for source in range(1, state.shape[0]):
        coupled = coupled + coupling[:, source, None, None, None] * state[source : source + 1]
    return (
        state
        - former
        + time_step * (advect - viscosity * laplace + vertical_mix * vertical + coupled)
    )


def local(base_state, base_old, fine_state, fine_old, coupling, patch_offsets, patch_group):
    groups = lax.axis_size("gx")
    members = lax.axis_size("gy")
    row_block = lax.axis_index("gx")
    col_block = lax.axis_index("gy")
    fields, levels, block_x, block_y = base_state.shape
    grid_x = block_x * groups
    fine_rows = fine_state.shape[3]
    fine_cols = fine_state.shape[4]
    zero = jnp.zeros((), jnp.int32)
    padded = padded_2(base_state, (("gx", 2), ("gy", 3)), 1)
    base_tend = tendency(padded, base_state, base_old, coupling, 1.0)
    owner = (patch_group[None, :] == jnp.arange(groups, dtype=jnp.int32)[:, None]).astype(jnp.int32)
    placed = jnp.sum(owner[:, :, None] * patch_offsets[None, :, :], axis=1)
    mine = lax.dynamic_index_in_dim(placed, row_block, 0, keepdims=False)
    start_x = mine[0]
    start_y = mine[1]
    row_local = jnp.stack([placed[:, 0] - 1, placed[:, 0] + PC], axis=1) - row_block * block_x
    row_inside = ((row_local >= 0) & (row_local < block_x)).astype(jnp.float32)
    picked_rows = jnp.take(base_state, jnp.clip(row_local, 0, block_x - 1).reshape(-1), axis=2)
    row_slots = (
        picked_rows.reshape(fields, levels, groups, 2, block_y) * row_inside[None, None, :, :, None]
    )
    row_slots = jnp.moveaxis(row_slots, 2, 0)
    col_local = jnp.stack([placed[:, 1] - 1, placed[:, 1] + PC], axis=1) - col_block * block_y
    col_inside = ((col_local >= 0) & (col_local < block_y)).astype(jnp.float32)
    picked_cols = jnp.take(base_state, jnp.clip(col_local, 0, block_y - 1).reshape(-1), axis=3)
    col_slots = (
        picked_cols.reshape(fields, levels, block_x, groups, 2) * col_inside[None, None, None, :, :]
    )
    col_slots = jnp.transpose(col_slots, (3, 0, 1, 4, 2))
    received_rows, received_cols = (
        lax.all_to_all(row_slots, "gx", split_axis=0, concat_axis=0, tiled=True),
        lax.all_to_all(col_slots, "gx", split_axis=0, concat_axis=0, tiled=True),
    )
    rows_part = jnp.sum(received_rows, axis=0)
    cols_part = jnp.transpose(received_cols, (1, 2, 3, 0, 4)).reshape(fields, levels, 2, grid_x)
    cycle_rows, cycle_stack = (
        lax.all_gather(rows_part, "gy", axis=3, tiled=True),
        lax.all_gather(cols_part[None], "gy", axis=0, tiled=True),
    )
    cycle_cols = jnp.sum(cycle_stack, axis=0)
    across_fine = start_y + jnp.arange(fine_cols, dtype=jnp.int32) // RATIO
    edges = jnp.take(cycle_rows, across_fine, axis=3)
    down_fine = start_x + (col_block * fine_rows + jnp.arange(fine_rows, dtype=jnp.int32)) // RATIO
    sides = jnp.take(cycle_cols, down_fine, axis=3)
    fine = fine_state[:, :, 0]
    former = fine_old[:, :, 0]
    halo_rows = padded_2(fine, (("gy", 2),), 1)
    first = jnp.where(col_block == 0, edges[:, :, 0:1], halo_rows[:, :, :1])
    last = jnp.where(col_block == members - 1, edges[:, :, 1:2], halo_rows[:, :, -1:])
    middle = jnp.concatenate([first, halo_rows[:, :, 1:-1], last], axis=2)
    corner = jnp.zeros((fields, levels, 1, 1), jnp.float32)
    left_col = jnp.concatenate([corner, sides[:, :, 0][..., None], corner], axis=2)
    right_col = jnp.concatenate([corner, sides[:, :, 1][..., None], corner], axis=2)
    padded_fine = jnp.concatenate([left_col, middle, right_col], axis=3)
    fine_res = tendency(padded_fine, fine, former, coupling, float(RATIO))
    piece_rows = fine_rows // RATIO
    piece = fine_res.reshape(fields, levels, piece_rows, RATIO, PC, RATIO).mean(axis=(3, 5))
    restricted = lax.all_gather(piece, "gy", axis=2, tiled=True)
    target = col_block * block_y + jnp.arange(block_y, dtype=jnp.int32) - start_y
    valid = ((target >= 0) & (target < PC)).astype(jnp.float32)
    placed_block = jnp.take(restricted, jnp.clip(target, 0, PC - 1), axis=3) * valid
    contrib = lax.dynamic_update_slice(
        jnp.zeros((fields, levels, grid_x, block_y), jnp.float32),
        placed_block,
        (zero, zero, start_x, zero),
    )
    covered_sum = lax.psum_scatter(contrib, "gx", scatter_dimension=2, tiled=True)
    rows_here = row_block * block_x + jnp.arange(block_x, dtype=jnp.int32)
    cols_here = col_block * block_y + jnp.arange(block_y, dtype=jnp.int32)
    inside_x = (
        (patch_offsets[:, 0:1] <= rows_here[None, :])
        & (rows_here[None, :] < patch_offsets[:, 0:1] + PC)
    ).astype(jnp.float32)
    inside_y = (
        (patch_offsets[:, 1:2] <= cols_here[None, :])
        & (cols_here[None, :] < patch_offsets[:, 1:2] + PC)
    ).astype(jnp.float32)
    covered = jnp.dot(inside_x.T, inside_y, precision=lax.Precision.HIGHEST) > 0.5
    base_out = jnp.where(covered[None, None], covered_sum, base_tend)
    base_sq = jnp.sum(jnp.where(covered[None, None], 0.0, base_tend * base_tend))
    fine_sq = jnp.sum(fine_res * fine_res) / (RATIO * RATIO)
    totals = lax.psum((base_sq, fine_sq), ("gx", "gy"))
    residual_norm = jnp.sqrt(totals[0] + totals[1])
    return (base_out, fine_res[:, :, None], residual_norm)


def solution(mesh):
    placed = (
        P(None, None, "gx", "gy"),
        P(None, None, "gx", "gy"),
        P(None, None, "gx", "gy", None),
        P(None, None, "gx", "gy", None),
        P(),
        P(),
        P(),
    )
    return jax.shard_map(
        local,
        mesh=mesh,
        in_specs=placed,
        out_specs=(P(None, None, "gx", "gy"), P(None, None, "gx", "gy", None), P()),
        check_vma=False,
    )
```

profile of v0, /device:TPU:0, one launch (start us, length us, event | category | flops | bytes accessed | tf_op | source)
XLA Modules:
  0.0 381.6 jit_solution(6572163703800557959)
XLA Ops:
  7.2 2.1 copy.314
  11.3 3.0 collective-permute-start.1
  17.7 3.2 copy.243
  20.9 2.3 gather_fusion.2
  28.4 7.3 %all-to-all-start.1 = ((f32[8,1,4096]{2,1,0:T(1,128)}), f32[8,1,4096]{2,1,0:T(1,128)}, u32[]{:S(2)}, u32[]{:S(2)}) async-start(f32[8,1,4096]{2,1,0:T(1,128)} %reshape.349), calls=%async_computation.1 | async-start | bytes 262144 | tf_op jit(solution)/shard_map/all_to_all | solution.py:82
  35.7 3.2 fusion.31
  45.4 2.5 gather_fusion
  64.6 6.1 %all-to-all-start = ((f32[8,4,8,2,128]{4,3,2,1,0:T(2,128)}), f32[8,4,8,2,128]{4,3,2,1,0:T(2,128)S(1)}, u32[]{:S(2)}, u32[]{:S(2)}) async-start(f32[8,4,8,2,128]{4,3,2,1,0:T(2,128)} %fusion.4), calls=%async_computation | async-start | bytes 524288 | tf_op jit(solution)/shard_map/all_to_all | solution.py:81
  71.3 2.5 reduce.10
  79.0 8.7 %all_gather.10 = f32[4,4,8,2,512]{4,2,3,1,0:T(8,128)} all-gather(f32[1,4,8,2,512]{4,2,3,1,0:T(8,128)} %broadcast_in_dim_reshape.3), channel_id=1, replica_groups=mesh['gx'=8,'gy'=4] {'gy'}, dimensions={0}, use_global_device_ids=true | all-gather | bytes 655360 | tf_op jit(solution)/shard_map/all_gather | solution.py:88
  89.5 2.5 copy.248
  92.0 3.2 gather_fusion.3
  97.7 3.6 copy.253
  101.3 3.5 copy.251
  105.9 17.6 %all_gather.9 = f32[4,8,2,512]{1,0,3,2:T(4,128)} all-gather(f32[4,8,2,128]{1,0,3,2:T(4,128)} %copy.233), channel_id=1, replica_groups=mesh['gx'=8,'gy'=4] {'gy'}, dimensions={3}, use_global_device_ids=true | all-gather | bytes 163840 | tf_op jit(solution)/shard_map/all_gather | solution.py:87
  123.4 4.1 %gather_fusion.1 = f32[264,4,8,2]{2,1,3,0:T(4,128)} fusion(f32[4,8,2,512]{1,0,3,2:T(4,128)} %all_gather.9, s32[1024]{0:T(1024)S(1)} %copy-done.8), kind=kCustom, calls=%fused_computation.1 | custom fusion | bytes 136224 | tf_op jit(solution)/shard_map/jit(_take)/gather | solution.py:92
  127.6 2.0 select_bitcast_fusion
  129.6 2.4 slice_select_fusion
  134.5 12.1 %multiply_reduce_fusion = (f32[]{:T(128)}, f32[4,8,66,264]{3,1,2,0:T(8,128)}) fusion(f32[8,66,264]{2,0,1:T(8,128)} %get-tuple-element.33, f32[4]{0:T(128)S(1)} %copy-done.13, f32[8,66,264]{2,0,1:T(8,128)} %get-tuple-element.31, f32[4]{0:T(128)S(1)} %copy-done.14, f32[4]{0:T(128)S(1)} %copy-done.12, f32[4]{0:T(128)S(1)} %copy-done.11, ...), kind=kLoop, calls=%fused_computation.17 | loop fusion | flops 22860288 | bytes 12908996 | tf_op jit(solution)/shard_map/reduce_sum | solution.py:131
  146.7 27.0 %copy.256 = f32[4,8,66,264]{1,0,3,2:T(4,128)} copy(f32[4,8,66,264]{3,1,2,0:T(8,128)} %get-tuple-element.23) | data formatting | bytes 4460544 | tf_op jit(solution)/shard_map/add | solution.py:43
  173.6 17.4 %reduce_sum.57 = f32[4,8,22,88]{1,0,3,2:T(4,128)} reduce(f32[4,8,22,3,88,3]{1,0,5,4,3,2:T(4,128)} %bitcast.80, f32[]{:T(128)} %constant.68.clone.1), dimensions={3,5}, to_apply=%region_3.4 | reduce | flops 495616 | bytes 2478084 | tf_op jit(solution)/shard_map/reduce_sum | solution.py:107
  191.0 3.5 copy.257
  194.6 12.4 %all_gather.11 = f32[4,8,88,88]{3,1,0,2:T(8,128)S(1)} all-gather(f32[4,8,22,88]{3,1,0,2:T(8,128)S(1)} %copy.258), channel_id=1, replica_groups=mesh['gx'=8,'gy'=4] {'gy'}, dimensions={2}, use_global_device_ids=true | all-gather | bytes 1239040 | tf_op jit(solution)/shard_map/all_gather | solution.py:108
  208.1 2.3 gather_fusion.4
  212.3 2.1 copy.260
  214.4 4.3 %broadcast_in_dim.93 = f32[4,8,512,128]{3,1,0,2:T(8,128)} broadcast(f32[]{:T(128)} %constant.68.clone.1), dimensions={} | broadcast | bytes 8388612 | tf_op jit(solution)/shard_map/broadcast_in_dim | solution.py:113
  222.5 4.8 %collective-permute-start.3 = (f32[4,8,1,128]{3,1,2,0:T(8,128)S(1)}, f32[4,8,1,128]{3,1,2,0:T(8,128)S(1)}, u32[]{:S(2)}, u32[]{:S(2)}) collective-permute-start(f32[4,8,1,128]{3,1,2,0:T(8,128)S(1)} %bitcast.92), channel_id=1, source_target_pairs={{0,4},{4,8},{8,12},{12,16},{16,20},{20,24},{24,28},{1,5},{5,9},{9,... | collective-permute-start | bytes 49160 | tf_op jit(solution)/shard_map/ppermute | solution.py:20
  237.7 3.0 collective-permute-start.5
  247.6 8.6 %select_reduce_fusion = (f32[]{:T(128)}, f32[4,8,64,128]{3,1,0,2:T(8,128)}) fusion(pred[64,128]{1,0:T(8,128)(4,1)S(1)} %convolution_compare_fusion, f32[8,64,128]{2,0,1:T(8,128)} %copy.283, f32[4]{0:T(128)} %get-tuple-element.20, f32[8,64,128]{2,0,1:T(8,128)} %copy.282, f32[4]{0:T(128)} %get-tuple-element.21, f32[4]{0:T(128)S(1)} %copy-done.12, ...), kind=kLoop, calls=%fused_computation.32 | loop fusion | flops 10485759 | bytes 6087236 | tf_op jit(solution)/shard_map/reduce_sum | solution.py:130
  257.5 44.2 %psum.16 = f32[]{:T(128)} all-reduce(f32[]{:T(128)S(6)} %add.373), channel_id=1, replica_groups=mesh['gx'=8,'gy'=4] {'gx','gy'}, use_global_device_ids=true, to_apply=%region_6.7 | all-reduce | flops 1 | bytes 8 | tf_op jit(solution)/shard_map/psum | solution.py:132
  302.4 5.0 %copy.285 = f32[4,8,1,66,264]{4,2,3,1,0:T(1,128)} copy(f32[4,8,1,66,264]{4,1,3,2,0:T(8,128)S(1)} %bitcast.84) | data formatting | bytes 4460544
  307.4 62.8 %reduce-scatter.2.cloned.1.call-done = f32[4,8,64,128]{3,1,0,2:T(8,128)} async-done(((f32[4,8,512,128]{3,1,0,2:T(8,128)}), f32[4,8,64,128]{3,1,0,2:T(8,128)}) %reduce-scatter.2.cloned.1.call-update) | async-done | bytes 1048592 | tf_op jit(solution)/shard_map/reduce_scatter | solution.py:117
  (135 shorter events, 73.0 us)
Async XLA Ops:
  7.2 7.2 %copy-start.22 = (s32[8]{0:T(128)S(1)}, s32[8]{0:T(128)}, u32[]{:S(2)}) copy-start(s32[8]{0:T(128)} %param.13) | copy-start | bytes 100
  7.2 7.2 %copy-start.15 = (s32[8,2]{0,1:T(2,128)S(1)}, s32[8,2]{0,1:T(2,128)}, u32[]{:S(2)}) copy-start(s32[8,2]{0,1:T(2,128)} %param.12) | copy-start | bytes 196
  10.0 51.8 %collective-permute-start = (f32[4,8,1,264]{3,1,2,0:T(8,128)}, f32[4,8,1,264]{3,1,2,0:T(8,128)}, u32[]{:S(2)}, u32[]{:S(2)}) collective-permute-start(f32[4,8,1,264]{3,1,2,0:T(8,128)} %get-tuple-element.35), channel_id=1, source_target_pairs={{1,0},{2,1},{3,2},{5,4},{6,5},{7,6},{9,8},{10,9},{11,10},{13,12},{... | collective-permute-start | bytes 101384 | tf_op jit(solution)/shard_map/ppermute | solution.py:23
  11.3 52.3 %collective-permute-start.1 = (f32[4,8,1,264]{3,1,2,0:T(8,128)}, f32[4,8,1,264]{3,1,2,0:T(8,128)S(1)}, u32[]{:S(2)}, u32[]{:S(2)}) collective-permute-start(f32[4,8,1,264]{3,1,2,0:T(8,128)} %get-tuple-element.34), channel_id=1, source_target_pairs={{0,1},{1,2},{2,3},{4,5},{5,6},{6,7},{8,9},{9,10},{10,11},{12,13},{... | collective-permute-start | bytes 101384 | tf_op jit(solution)/shard_map/ppermute | solution.py:20
  14.5 0.5 copy-start.9
  28.4 36.2 %all-to-all-start.1 = ((f32[8,1,4096]{2,1,0:T(1,128)}), f32[8,1,4096]{2,1,0:T(1,128)}, u32[]{:S(2)}, u32[]{:S(2)}) async-start(f32[8,1,4096]{2,1,0:T(1,128)} %reshape.349), calls=%async_computation.1 | async-start | bytes 262144 | tf_op jit(solution)/shard_map/all_to_all | solution.py:82
  38.8 1.8 copy-start.10
  38.8 6.0 %copy-start.19 = (s32[16]{0:T(128)S(1)}, s32[16]{0:T(128)}, u32[]{:S(2)}) copy-start(s32[16]{0:T(128)} %get-tuple-element.68) | copy-start | bytes 196
  64.6 30.6 %copy-start.21 = (pred[66]{0:T(512)(128)(4,1)S(1)}, pred[66]{0:T(512)(128)(4,1)}, u32[]{:S(2)}) copy-start(pred[66]{0:T(512)(128)(4,1)} %compare_and_fusion.1) | copy-start | bytes 202
  64.6 40.2 %all-to-all-start = ((f32[8,4,8,2,128]{4,3,2,1,0:T(2,128)}), f32[8,4,8,2,128]{4,3,2,1,0:T(2,128)S(1)}, u32[]{:S(2)}, u32[]{:S(2)}) async-start(f32[8,4,8,2,128]{4,3,2,1,0:T(2,128)} %fusion.4), calls=%async_computation | async-start | bytes 524288 | tf_op jit(solution)/shard_map/all_to_all | solution.py:81
  70.7 299.5 %reduce-scatter.2.cloned.1.call-start = ((), (), s32[]{:S(2)}) async-start(), calls=%async_computation.3 | async-start | bytes 9437184 | tf_op jit(solution)/shard_map/reduce_scatter | solution.py:117
  97.0 26.4 %copy-start.8 = (s32[1024]{0:T(1024)S(1)}, s32[1024]{0:T(1024)}, u32[]{:S(2)}) copy-start(s32[1024]{0:T(1024)} %pad_clamp_fusion.3) | copy-start | bytes 12292
  97.0 30.5 %copy-start.20 = (pred[264]{0:T(512)(128)(4,1)S(1)}, pred[264]{0:T(512)(128)(4,1)}, u32[]{:S(2)}) copy-start(pred[264]{0:T(512)(128)(4,1)} %compare_and_fusion.3) | copy-start | bytes 796
  127.5 7.0 %copy-start.11 = (f32[4]{0:T(128)S(1)}, f32[4]{0:T(128)}, u32[]{:S(2)}) copy-start(f32[4]{0:T(128)} %get-tuple-element.18) | copy-start | bytes 52
  127.5 7.0 %copy-start.12 = (f32[4]{0:T(128)S(1)}, f32[4]{0:T(128)}, u32[]{:S(2)}) copy-start(f32[4]{0:T(128)} %get-tuple-element.19) | copy-start | bytes 52
  127.5 7.0 %copy-start.13 = (f32[4]{0:T(128)S(1)}, f32[4]{0:T(128)}, u32[]{:S(2)}) copy-start(f32[4]{0:T(128)} %get-tuple-element.20) | copy-start | bytes 52
  127.5 7.0 %copy-start.14 = (f32[4]{0:T(128)S(1)}, f32[4]{0:T(128)}, u32[]{:S(2)}) copy-start(f32[4]{0:T(128)} %get-tuple-element.21) | copy-start | bytes 52
  207.0 3.4 copy-start.17
  207.0 3.4 copy-start.18
  214.4 4.3 %copy-start.3 = (f32[4,8,88,128]{3,1,0,2:T(8,128)S(1)}, f32[4,8,88,128]{3,1,0,2:T(8,128)}, u32[]{:S(2)}) copy-start(f32[4,8,88,128]{3,1,0,2:T(8,128)} %copy.260) | copy-start | bytes 4325380
  220.0 1.2 copy-start.1
  220.0 8.0 %copy-start.16 = (s32[8,2]{0,1:T(2,128)S(1)}, s32[8,2]{0,1:T(2,128)}, u32[]{:S(2)}) copy-start(s32[8,2]{0,1:T(2,128)} %param.12) | copy-start | bytes 196
  221.2 9.5 %collective-permute-start.2 = (f32[4,8,1,128]{3,1,2,0:T(8,128)S(1)}, f32[4,8,1,128]{3,1,2,0:T(8,128)S(1)}, u32[]{:S(2)}, u32[]{:S(2)}) collective-permute-start(f32[4,8,1,128]{3,1,2,0:T(8,128)S(1)} %bitcast.93), channel_id=1, source_target_pairs={{4,0},{8,4},{12,8},{16,12},{20,16},{24,20},{28,24},{5,1},{9,5},{13... | collective-permute-start | bytes 49160 | tf_op jit(solution)/shard_map/ppermute | solution.py:23
  222.5 8.2 %collective-permute-start.3 = (f32[4,8,1,128]{3,1,2,0:T(8,128)S(1)}, f32[4,8,1,128]{3,1,2,0:T(8,128)S(1)}, u32[]{:S(2)}, u32[]{:S(2)}) collective-permute-start(f32[4,8,1,128]{3,1,2,0:T(8,128)S(1)} %bitcast.92), channel_id=1, source_target_pairs={{0,4},{4,8},{8,12},{12,16},{16,20},{20,24},{24,28},{1,5},{5,9},{9,... | collective-permute-start | bytes 49160 | tf_op jit(solution)/shard_map/ppermute | solution.py:20
  227.9 2.9 copy-start.2
  230.8 10.2 %copy-start.7 = (f32[8,64,128]{2,1,0:T(8,128)S(1)}, f32[8,64,128]{2,1,0:T(8,128)}, u32[]{:S(2)}) copy-start(f32[8,64,128]{2,1,0:T(8,128)} %get-tuple-element.44) | copy-start | bytes 786436
  230.8 10.3 %copy-start.6 = (f32[8,64,128]{2,1,0:T(8,128)S(1)}, f32[8,64,128]{2,1,0:T(8,128)}, u32[]{:S(2)}) copy-start(f32[8,64,128]{2,1,0:T(8,128)} %get-tuple-element.45) | copy-start | bytes 786436
  230.8 11.2 %copy-start.5 = (f32[8,64,128]{2,1,0:T(8,128)S(1)}, f32[8,64,128]{2,1,0:T(8,128)}, u32[]{:S(2)}) copy-start(f32[8,64,128]{2,1,0:T(8,128)} %get-tuple-element.47) | copy-start | bytes 786436
  230.8 12.0 %copy-start.4 = (f32[8,64,128]{2,1,0:T(8,128)S(1)}, f32[8,64,128]{2,1,0:T(8,128)}, u32[]{:S(2)}) copy-start(f32[8,64,128]{2,1,0:T(8,128)} %get-tuple-element.46) | copy-start | bytes 786436
  234.5 9.2 %collective-permute-start.4 = (f32[4,8,66,1]{2,1,3,0:T(8,128)S(1)}, f32[4,8,66,1]{2,1,3,0:T(8,128)S(1)}, u32[]{:S(2)}, u32[]{:S(2)}) collective-permute-start(f32[4,8,66,1]{2,1,3,0:T(8,128)S(1)} %copy.274), channel_id=1, source_target_pairs={{1,0},{2,1},{3,2},{5,4},{6,5},{7,6},{9,8},{10,9},{11,10},{13,12},{... | collective-permute-start | bytes 25352 | tf_op jit(solution)/shard_map/ppermute | solution.py:23
  237.7 8.0 %collective-permute-start.5 = (f32[4,8,66,1]{2,1,3,0:T(8,128)S(1)}, f32[4,8,66,1]{2,1,3,0:T(8,128)S(1)}, u32[]{:S(2)}, u32[]{:S(2)}) collective-permute-start(f32[4,8,66,1]{2,1,3,0:T(8,128)S(1)} %copy.276), channel_id=1, source_target_pairs={{0,1},{1,2},{2,3},{4,5},{5,6},{6,7},{8,9},{9,10},{10,11},{12,13},{... | collective-permute-start | bytes 25352 | tf_op jit(solution)/shard_map/ppermute | solution.py:20
  247.6 54.8 %copy-start = (f32[4,8,66,264]{3,1,2,0:T(8,128)S(1)}, f32[4,8,66,264]{3,1,2,0:T(8,128)}, u32[]{:S(2)}) copy-start(f32[4,8,66,264]{3,1,2,0:T(8,128)} %get-tuple-element.23) | copy-start | bytes 6690820
Sparse Core Ops, SparseCore 0:
  220.1 150.0 reduce-scatter.1
where the time goes:
time: 385 us; the launch traced here: 382 us
  local copies, waits for them, and re-layouts  120 us (31%)
  blocking collectives  83 us (22%)
  other arithmetic  67.7 us (18%)
  waiting for transfers between devices  62.9 us (16%)
  starting transfers between devices  28.1 us (7%)
  between operations  19.4 us (5%)
    reduce_scatter x1, waiting for transfers between devices, local(): lax.psum_scatter(contrib, 'gx', scatter_dimension=2, tiled=True)  62.8 us
    psum x1, blocking collectives, local(): totals = lax.psum((base_sq, fine_sq), ('gx', 'gy'))  44.2 us
    add x1, local copies, waits for them, and re-layouts, tendency(): state - former  27 us
    all_gather x1, blocking collectives, local(): lax.all_gather(rows_part, 'gy', axis=3, tiled=True)  17.6 us
    reduce_sum x1, other arithmetic, local(): fine_res.reshape(fields, levels, piece_rows, RATIO, PC, RATIO)  17.4 us
    unnamed x53, local copies, waits for them, and re-layouts  16.9 us
    all_gather x1, blocking collectives, local(): restricted = lax.all_gather(piece, 'gy', axis=2, tiled=True)  12.4 us
    reduce_sum x1, other arithmetic, local(): fine_sq = jnp.sum(fine_res * fine_res) / (RATIO * RATIO)  12.1 us
  transfers between devices with their start and end apart: 9, of which 1 were waited for; matrix products, arithmetic and copies ran while one was open for 25% of the time, Pallas kernels for 0%

commit v1 on v0

v1 whole, which is shorter than its diff:
```python
import functools

import jax
import jax.numpy as jnp
from jax import lax
from jax.experimental import pallas as pl
from jax.experimental.pallas import tpu as pltpu
from jax.sharding import PartitionSpec as P

PC = 88
RATIO = 3

time_step = 0.1
viscosity = 0.2
vertical_mix = 0.5

F32 = jnp.float32
BF16 = jnp.bfloat16
HIGH = lax.Precision.HIGHEST
MESH = pl.DeviceIdType.MESH
VMEM = pl.BlockSpec(memory_space=pltpu.VMEM)
SMEM = pl.BlockSpec(memory_space=pltpu.SMEM)


def params(**more):
    return pltpu.CompilerParams(vmem_limit_bytes=58 * 1024 * 1024, **more)


def iota(shape, dim):
    return lax.broadcasted_iota(jnp.int32, shape, dim)


def comm_kernel(plan, axes, inner, *refs):
    count = len(plan)
    sources, targets = refs[:count], refs[count : 2 * count]
    send_sem, recv_sem, local_sem = refs[2 * count :]
    barrier = pltpu.get_barrier_semaphore()
    total = 0
    for axis, size in axes.items():
        me = lax.axis_index(axis)
        for step in range(1, size):
            pl.semaphore_signal(
                barrier, inc=1, device_id={axis: lax.rem(me + step, size)}, device_id_type=MESH
            )
        total += size - 1
    pl.semaphore_wait(barrier, total)
    used = [0]
    waiting = []

    def send(source, target, axis, peer):
        slot = used[0]
        used[0] += 1
        copy = pltpu.make_async_remote_copy(
            src_ref=source,
            dst_ref=target,
            send_sem=send_sem.at[slot],
            recv_sem=recv_sem.at[slot],
            device_id={axis: peer},
            device_id_type=MESH,
        )
        copy.start()
        return copy

    relays = []
    local = []
    for index, (mode, axis) in enumerate(plan):
        source, target = sources[index], targets[index]
        size = axes[axis]
        me = lax.axis_index(axis)
        if mode == "shift":
            up, down = lax.rem(me + 1, size), lax.rem(me + size - 1, size)
            waiting.append(send(source.at[1], target.at[0], axis, up))
            waiting.append(send(source.at[0], target.at[1], axis, down))
            continue
        own = pltpu.make_async_copy(
            source.at[me] if mode == "exchange" else source, target.at[me], local_sem.at[index]
        )
        own.start()
        local.append(own)
        if mode == "relay":
            outer = size // inner
            high, low = lax.div(me, inner), lax.rem(me, inner)
            for step in range(1, outer):
                peer = lax.rem(high + step, outer) * inner + low
                origin = lax.rem(high + outer - step, outer) * inner + low
                relays.append((send(source, target.at[me], axis, peer), target, origin))
            for hop in range(1, inner):
                peer = high * inner + lax.rem(low + hop, inner)
                waiting.append(send(source, target.at[me], axis, peer))
            continue
        for step in range(1, size):
            peer = lax.rem(me + step, size)
            part = source.at[peer] if mode == "exchange" else source
            waiting.append(send(part, target.at[me], axis, peer))
    for copy, target, origin in relays:
        copy.wait_recv()
        me = lax.axis_index("gx")
        high, low = lax.div(me, inner), lax.rem(me, inner)
        for hop in range(1, inner):
            peer = high * inner + lax.rem(low + hop, inner)
            waiting.append(send(target.at[origin], target.at[origin], "gx", peer))
    for copy, _, _ in relays:
        copy.wait_send()
    for copy in waiting:
        copy.wait()
    for copy in local:
        copy.wait()


def communicate(name, ident, sizes, plan, *arrays):
    axes = {axis: sizes[axis] for _, axis in plan}
    inner = 1
    while (2 * inner) ** 2 <= sizes["gx"]:
        inner *= 2
    slots = 0
    shapes = []
    for (mode, axis), array in zip(plan, arrays):
        size = axes[axis]
        if mode == "shift":
            slots += 2
            shapes.append(array.shape)
        elif mode == "exchange":
            slots += size - 1
            shapes.append(array.shape)
        else:
            slots += size - 1
            shapes.append((size, *array.shape))
    return pl.pallas_call(
        functools.partial(comm_kernel, plan, axes, inner),
        out_shape=[jax.ShapeDtypeStruct(s, F32) for s in shapes],
        in_specs=[VMEM] * len(plan),
        out_specs=[VMEM] * len(plan),
        scratch_shapes=[
            pltpu.SemaphoreType.DMA((slots,)),
            pltpu.SemaphoreType.DMA((slots,)),
            pltpu.SemaphoreType.DMA((len(plan),)),
        ],
        compiler_params=params(collective_id=ident, has_side_effects=True),
        name=name,
    )(*arrays)


def prepare_kernel(groups, last_row, rows_ref, cols_ref, base, top, bottom, cyc, brow, bcol, frow):
    fields, levels, block_x, block_y = base.shape
    pick_rows = (iota((2 * groups, block_x), 1) == rows_ref[...]).astype(F32)
    pick_cols = (iota((2 * groups + 8, block_y), 1) == cols_ref[...]).astype(F32)
    for z in range(levels):
        for f in range(fields):
            q = base[f, z]
            flat = z * fields + f
            found = jnp.dot(pick_rows, q, precision=HIGH, preferred_element_type=F32)
            side = lax.dot_general(
                pick_cols, q, (((1,), (1,)), ((), ())), precision=HIGH, preferred_element_type=F32
            )
            both = jnp.concatenate([side[:groups], side[groups : 2 * groups]], axis=1)
            for g in range(groups):
                high = z * 2 * fields + f
                cyc[g, high : high + 1] = found[g : g + 1]
                cyc[g, high + fields : high + fields + 1] = found[groups + g : groups + g + 1]
                at = 2 * fields * levels + flat
                cyc[g, at : at + 1] = both[g : g + 1]
            brow[0, flat : flat + 1] = q[:1]
            brow[1, flat : flat + 1] = q[block_x - 1 :]
            bcol[0, flat : flat + 1] = side[2 * groups : 2 * groups + 1]
            bcol[1, flat : flat + 1] = side[2 * groups + 1 : 2 * groups + 2]
            frow[0, flat : flat + 1] = top[f, z, 0, :1]
            frow[1, flat : flat + 1] = bottom[f, z, 0, last_row : last_row + 1]


def cycle_kernel(groups, fields, block_x, meta, got, piece):
    half = got.shape[1] * 2 // 3
    width = got.shape[2]
    row_block = meta[2 * groups]
    start = meta[2 * row_block]
    rows = got[0, :half]
    sides = None
    for b in range(groups):
        if b:
            rows = rows + got[b, :half]
        lane = iota((width, 2 * width), 0)
        slot = iota((width, 2 * width), 1)
        low = (lane < block_x) & (lane + b * block_x == slot + start) & (slot < PC)
        high = (
            (lane >= block_x)
            & (lane - block_x + b * block_x == slot - width + start)
            & (slot >= width)
            & (slot < width + PC)
        )
        term = jnp.dot(
            got[b, half:], (low | high).astype(F32), precision=HIGH, preferred_element_type=F32
        )
        sides = term if sides is None else sides + term
    piece[:half] = rows
    for z in range(half // (2 * fields)):
        at = half + z * 2 * fields
        piece[at : at + fields] = sides[z * fields : (z + 1) * fields, :width]
        piece[at + fields : at + 2 * fields] = sides[z * fields : (z + 1) * fields, width:]


def level(state, former, coupling, z, first, last, left, right, inverse):
    fields, levels = len(first), state(None, None)
    q = [state(f, z) for f in range(fields)]
    out = []
    for f in range(fields):
        north = jnp.concatenate([q[f][1:], last[f]], axis=0)
        south = jnp.concatenate([first[f], q[f][:-1]], axis=0)
        east = jnp.concatenate([q[f][:, 1:], right[f]], axis=1)
        west = jnp.concatenate([left[f], q[f][:, :-1]], axis=1)
        advect = (q[0] * (north - south) + q[1] * (east - west)) * (0.5 * inverse)
        laplace = (north + south + east + west - 4.0 * q[f]) * (inverse * inverse)
        upper = jnp.where(z < levels - 1, state(f, jnp.minimum(z + 1, levels - 1)), 0.0)
        lower = jnp.where(z > 0, state(f, jnp.maximum(z - 1, 0)), 0.0)
        vertical = 2.0 * q[f] - upper - lower
        coupled = coupling[f, 0] * q[0]
        for g in range(1, fields):
            coupled = coupled + coupling[f, g] * q[g]
        out.append(
            q[f]
            - former(f)
            + time_step * (advect - viscosity * laplace + vertical_mix * vertical + coupled)
        )
    return out


def fold(values):
    total = jnp.sum(values, axis=0, keepdims=True)
    acc = total[:, :128]
    for at in range(128, values.shape[1], 128):
        part = total[:, at : at + 128]
        if part.shape[1] < 128:
            part = jnp.concatenate([part, jnp.zeros((1, 128 - part.shape[1]), F32)], axis=1)
        acc = acc + part
    return acc


def fine_kernel(
    groups, members, meta, coupling, gath, halo, state, old, res, rest, sq, edge, side, fit, thin
):
    z = pl.program_id(0)
    fields, levels = state.shape[:2]
    fine_rows, fine_cols = state.shape[3:]
    piece = fine_rows // RATIO
    block_y = gath.shape[2]
    row_block = meta[2 * groups]
    col_block = meta[2 * groups + 1]
    start_y = meta[2 * row_block + 1]
    half = 2 * fields * levels

    @pl.when(z == 0)
    def _():
        sq[...] = jnp.zeros_like(sq)
        lane = iota((block_y, fine_cols), 0)
        fine = iota((block_y, fine_cols), 1) // RATIO
        rows = None
        cols = gath[0, half:]
        for b in range(members):
            pick = (lane + b * block_y == fine + start_y).astype(F32)
            term = jnp.dot(gath[b, :half], pick, precision=HIGH, preferred_element_type=F32)
            rows = term if rows is None else rows + term
            if b:
                cols = cols + gath[b, half:]
        edge[...] = rows
        pick = iota((128, 128), 0) == piece * col_block + iota((128, 128), 1) // RATIO
        side[...] = jnp.dot(cols, pick.astype(F32), precision=HIGH, preferred_element_type=F32)
        cell = iota((fine_cols, 128), 0) // RATIO + start_y
        fit[...] = (lax.rem(cell, block_y) == iota((fine_cols, 128), 1)).astype(F32).astype(BF16)

    at = pl.multiple_of(z * 2 * fields, 8)
    edges = edge[pl.ds(at, 2 * fields)]
    turned = jnp.transpose(side[pl.ds(at, 2 * fields)])
    first, last, left, right = [], [], [], []
    for f in range(fields):
        above = halo[0, pl.ds(z * fields + f, 1)]
        below = halo[1, pl.ds(z * fields + f, 1)]
        first.append(jnp.where(col_block == 0, edges[f : f + 1], above))
        last.append(jnp.where(col_block == members - 1, edges[fields + f : fields + f + 1], below))
        left.append(turned[:fine_rows, f : f + 1])
        right.append(turned[:fine_rows, fields + f : fields + f + 1])

    def cell(f, at):
        return levels if f is None else state[f, at, 0]

    got = level(
        cell, lambda f: old[f, 0, 0], coupling, z, first, last, left, right, float(RATIO)
    )
    squares = None
    for f in range(fields):
        res[f, 0, 0] = got[f]
        squares = got[f] * got[f] if f == 0 else squares + got[f] * got[f]
        major = got[f].astype(BF16)
        minor = (got[f] - major.astype(F32)).astype(BF16)
        narrow = jnp.dot(major, fit[...], preferred_element_type=F32) + jnp.dot(
            minor, fit[...], preferred_element_type=F32
        )
        thin[f] = narrow * (1.0 / (RATIO * RATIO))
        total = thin[f, pl.ds(0, piece, stride=RATIO), :]
        for k in range(1, RATIO):
            total = total + thin[f, pl.ds(k, piece, stride=RATIO), :]
        rest[f, pl.ds(z, piece, stride=levels), :] = total
    sq[0:1] += fold(squares) * (1.0 / (RATIO * RATIO))


def base_kernel(groups, members, meta, coupling, rows, cols, state, old, res, sq):
    z = pl.program_id(0)
    fields, levels, block_x, block_y = state.shape
    row_block = meta[2 * groups]
    col_block = meta[2 * groups + 1]

    @pl.when(z == 0)
    def _():
        sq[...] = jnp.zeros_like(sq)

    first, last, left, right = [], [], [], []
    for f in range(fields):
        at = z * fields + f
        first.append(jnp.where(row_block > 0, rows[0, pl.ds(at, 1)], 0.0))
        last.append(jnp.where(row_block < groups - 1, rows[1, pl.ds(at, 1)], 0.0))
        left.append(jnp.where(col_block > 0, cols[0, pl.ds(at, 1)], 0.0))
        right.append(jnp.where(col_block < members - 1, cols[1, pl.ds(at, 1)], 0.0))
    turned = jnp.transpose(jnp.concatenate(left + right, axis=0))
    left = [turned[:, f : f + 1] for f in range(fields)]
    right = [turned[:, fields + f : fields + f + 1] for f in range(fields)]

    def cell(f, at):
        return levels if f is None else state[f, at]

    got = level(cell, lambda f: old[f, 0], coupling, z, first, last, left, right, 1.0)
    x = iota((block_x, block_y), 0) + row_block * block_x
    y = iota((block_x, block_y), 1) + col_block * block_y
    covered = jnp.zeros((block_x, block_y), jnp.bool_)
    for g in range(groups):
        dx, dy = x - meta[2 * g], y - meta[2 * g + 1]
        covered = covered | ((dx >= 0) & (dx < PC) & (dy >= 0) & (dy < PC))
    squares = None
    for f in range(fields):
        res[f, 0] = got[f]
        squares = got[f] * got[f] if f == 0 else squares + got[f] * got[f]
    sq[0:1] += fold(jnp.where(covered, 0.0, squares))


def sort_kernel(groups, members, block_x, meta, got, sums, slots, total):
    fields, depth, block_y = got.shape[1:]
    levels = depth * RATIO // (PC * RATIO // members)
    piece = depth // levels
    row_block = meta[2 * groups]
    col_block = meta[2 * groups + 1]
    acc = sums[0]
    for g in range(1, groups):
        acc = acc + sums[g]
    total[...] = acc
    for g in range(groups):
        begin = meta[2 * g] + col_block * piece - row_block * block_x
        start_y = meta[2 * g + 1]
        here = (begin < block_x) & (begin + piece > 0)
        for b in range(members):
            shift = start_y - b * block_y

            @pl.when(here & (shift < block_y) & (shift + PC > 0))
            def _():
                lane = iota((depth, block_y), 1)
                inside = (lane >= shift) & (lane < shift + PC)
                for f in range(fields):
                    slots[b, f] = jnp.where(inside, got[g, f], slots[b, f])


def place_kernel(groups, members, meta, tend, got, sums, out, norm, laid):
    fields, levels, block_x, block_y = tend.shape
    depth = got.shape[2]
    piece = depth // levels
    row_block = meta[2 * groups]
    col_block = meta[2 * groups + 1]
    acc = sums[0]
    for b in range(1, members):
        acc = acc + sums[b]
    norm[...] = jnp.sqrt(jnp.sum(acc, keepdims=True))
    x = iota((block_x, block_y), 0) + row_block * block_x
    y = iota((block_x, block_y), 1) + col_block * block_y
    covered = jnp.zeros((block_x, block_y), jnp.bool_)
    for g in range(groups):
        dx, dy = x - meta[2 * g], y - meta[2 * g + 1]
        covered = covered | ((dx >= 0) & (dx < PC) & (dy >= 0) & (dy < PC))
        begin = meta[2 * g] - row_block * block_x
        shift = meta[2 * g + 1] - col_block * block_y

        @pl.when((begin < block_x) & (begin + PC > 0) & (shift < block_y) & (shift + PC > 0))
        def _():
            lane = iota((levels, block_y), 1)
            inside = (lane >= shift) & (lane < shift + PC)

            def row(at, carry):
                patch_row = at - begin
                part = patch_row // piece
                source = pl.multiple_of((patch_row - part * piece) * levels, levels)
                target = pl.multiple_of(at * levels, levels)
                for f in range(fields):
                    laid[f, pl.ds(target, levels)] = jnp.where(
                        inside,
                        got[part, f, pl.ds(source, levels)],
                        laid[f, pl.ds(target, levels)],
                    )
                return carry

            lax.fori_loop(jnp.maximum(begin, 0), jnp.minimum(begin + PC, block_x), row, 0)

    for f in range(fields):
        for z in range(levels):
            out[f, z] = jnp.where(
                covered, laid[f, pl.ds(z, block_x, stride=levels), :], tend[f, z]
            )


def local(sizes, base_state, base_old, fine_state, fine_old, coupling, patch_offsets, patch_group):
    groups, members = sizes["gx"], sizes["gy"]
    row_block = lax.axis_index("gx")
    col_block = lax.axis_index("gy")
    fields, levels, block_x, block_y = base_state.shape
    fine_rows, fine_cols = fine_state.shape[3:]
    piece = fine_rows // RATIO
    flat = fields * levels
    owner = (patch_group[None, :] == jnp.arange(groups, dtype=jnp.int32)[:, None]).astype(jnp.int32)
    placed = jnp.sum(owner[:, :, None] * patch_offsets[None, :, :], axis=1)
    meta = jnp.concatenate([placed.reshape(-1), jnp.stack([row_block, col_block])])
    row_pick = jnp.concatenate([placed[:, 0] - 1, placed[:, 0] + PC]) - row_block * block_x
    col_pick = jnp.concatenate([placed[:, 1] - 1, placed[:, 1] + PC]) - col_block * block_y
    ends = jnp.array([0, block_y - 1, -1, -1, -1, -1, -1, -1], jnp.int32)
    col_pick = jnp.concatenate([col_pick, ends])

    def shape(*dims):
        return jax.ShapeDtypeStruct(dims, F32)

    tail = fine_rows - 1
    cyc, brow, bcol, frow = pl.pallas_call(
        functools.partial(prepare_kernel, groups, tail % 8),
        grid=(1,),
        out_shape=[
            shape(groups, 3 * flat, block_y),
            shape(2, flat, block_y),
            shape(2, flat, block_x),
            shape(2, flat, fine_cols),
        ],
        in_specs=[
            VMEM,
            VMEM,
            VMEM,
            pl.BlockSpec((fields, levels, 1, 8, fine_cols), lambda i: (0, 0, 0, 0, 0)),
            pl.BlockSpec((fields, levels, 1, 8, fine_cols), lambda i: (0, 0, 0, tail // 8, 0)),
        ],
        out_specs=[VMEM] * 4,
        compiler_params=params(),
        name="prepare",
    )(row_pick[:, None], col_pick[:, None], base_state, fine_state, fine_state)

    cyc, brow, bcol, frow = communicate(
        "edges",
        1,
        sizes,
        (("exchange", "gx"), ("shift", "gx"), ("shift", "gy"), ("shift", "gy")),
        cyc,
        brow,
        bcol,
        frow,
    )
    cycle = pl.pallas_call(
        functools.partial(cycle_kernel, groups, fields, block_x),
        out_shape=shape(4 * flat, block_y),
        in_specs=[SMEM, VMEM],
        out_specs=VMEM,
        compiler_params=params(),
        name="cycle",
    )(meta, cyc)
    (gath,) = communicate("members", 2, sizes, (("gather", "gy"),), cycle)

    slab = (fields, levels, 1, fine_rows, fine_cols)
    thin = (fields, 1, 1, fine_rows, fine_cols)
    fine_res, rest, fine_sq = pl.pallas_call(
        functools.partial(fine_kernel, groups, members),
        grid=(levels,),
        out_shape=[shape(*slab), shape(fields, piece * levels, 128), shape(8, 128)],
        in_specs=[
            SMEM,
            SMEM,
            VMEM,
            VMEM,
            pl.BlockSpec(slab, lambda z: (0, 0, 0, 0, 0)),
            pl.BlockSpec(thin, lambda z: (0, z, 0, 0, 0)),
        ],
        out_specs=[
            pl.BlockSpec(thin, lambda z: (0, z, 0, 0, 0)),
            pl.BlockSpec((fields, piece * levels, 128), lambda z: (0, 0, 0)),
            pl.BlockSpec((8, 128), lambda z: (0, 0)),
        ],
        scratch_shapes=[
            pltpu.VMEM((2 * flat, fine_cols), F32),
            pltpu.VMEM((2 * flat, 128), F32),
            pltpu.VMEM((fine_cols, 128), BF16),
            pltpu.VMEM((fields, fine_rows, 128), F32),
        ],
        compiler_params=params(),
        name="fine",
    )(meta, coupling, gath, frow, fine_state, fine_old)

    whole = (fields, levels, block_x, block_y)
    sheet = (fields, 1, block_x, block_y)
    tend, base_sq = pl.pallas_call(
        functools.partial(base_kernel, groups, members),
        grid=(levels,),
        out_shape=[shape(*whole), shape(8, 128)],
        in_specs=[
            SMEM,
            SMEM,
            VMEM,
            VMEM,
            pl.BlockSpec(whole, lambda z: (0, 0, 0, 0)),
            pl.BlockSpec(sheet, lambda z: (0, z, 0, 0)),
        ],
        out_specs=[
            pl.BlockSpec(sheet, lambda z: (0, z, 0, 0)),
            pl.BlockSpec((8, 128), lambda z: (0, 0)),
        ],
        compiler_params=params(),
        name="base",
    )(meta, coupling, brow, bcol, base_state, base_old)

    gathered, sums = communicate(
        "owners", 3, sizes, (("relay", "gx"), ("gather", "gx")), rest, fine_sq + base_sq
    )
    slots, total = pl.pallas_call(
        functools.partial(sort_kernel, groups, members, block_x),
        out_shape=[shape(members, fields, piece * levels, block_y), shape(8, 128)],
        in_specs=[SMEM, VMEM, VMEM],
        out_specs=[VMEM, VMEM],
        compiler_params=params(),
        name="sort",
    )(meta, gathered, sums)
    slots, sums = communicate(
        "columns", 4, sizes, (("exchange", "gy"), ("gather", "gy")), slots, total
    )
    base_out, norm = pl.pallas_call(
        functools.partial(place_kernel, groups, members),
        out_shape=[shape(*whole), shape(1, 1)],
        in_specs=[SMEM, VMEM, VMEM, VMEM],
        out_specs=[VMEM, VMEM],
        scratch_shapes=[pltpu.VMEM((fields, block_x * levels, block_y), F32)],
        compiler_params=params(),
        name="place",
    )(meta, tend, slots, sums)
    return (base_out, fine_res, norm[0, 0])


def solution(mesh):
    placed = (
        P(None, None, "gx", "gy"),
        P(None, None, "gx", "gy"),
        P(None, None, "gx", "gy", None),
        P(None, None, "gx", "gy", None),
        P(),
        P(),
        P(),
    )
    return jax.shard_map(
        functools.partial(local, dict(mesh.shape)),
        mesh=mesh,
        in_specs=placed,
        out_specs=(P(None, None, "gx", "gy"), P(None, None, "gx", "gy", None), P()),
        check_vma=False,
    )
```

time: 385 us -> 151 us (0.39)
  the two profiles are of different devices: /device:TPU:0 before, /device:TPU:29 now
where the time goes in v1:
time: 151 us
  Pallas kernels  134 us (89%)
  local copies, waits for them, and re-layouts  12 us (8%)
  other arithmetic  4.84 us (3%)
    pallas_call x4, Pallas kernels, communicate(): pl.pallas_call(functools.partial(comm_kernel, plan, axes, inner), out_sha...  99.4 us
    pallas_call x1, Pallas kernels, local(): pl.pallas_call(functools.partial(fine_kernel, groups, members), grid=(lev...  12.3 us
    unnamed x7, local copies, waits for them, and re-layouts  11.1 us
    pallas_call x1, Pallas kernels, local(): pl.pallas_call(functools.partial(base_kernel, groups, members), grid=(lev...  6.98 us
    pallas_call x1, Pallas kernels, local(): pl.pallas_call(functools.partial(prepare_kernel, groups, tail % 8), grid=...  5.09 us
    pallas_call x1, Pallas kernels, local(): pl.pallas_call(functools.partial(place_kernel, groups, members), out_shap...  4.17 us
    pallas_call x1, Pallas kernels, local(): pl.pallas_call(functools.partial(sort_kernel, groups, members, block_x),...  3.45 us

profile of v1, /device:TPU:29, one launch (start us, length us, event | category | flops | bytes accessed | tf_op | source)
XLA Modules:
  0.0 151.1 jit_solution(6226533016555550140)
XLA Ops:
  0.6 0.7 fusion
  1.3 0.8 multiply_reduce_fusion
  2.1 0.1 pad_add_fusion.1
  2.2 0.1 copy.43
  2.3 0.6 broadcast_subtract_fusion.rows_ref
  2.9 0.1 add_subtract_fusion
  3.0 0.7 add_bitcast_fusion
  3.7 0.7 copy.45.cols_ref
  4.4 4.0 %copy.46.top.bottom.state = f32[4,8,1,66,264]{4,3,2,1,0:T(8,128)} copy(f32[4,8,1,66,264]{4,2,3,1,0:T(1,128)} %param.10) | data formatting | bytes 4460544 | tf_op args[2]
  8.4 0.0 copy-start.1
  8.4 5.1 %prepare.1 = (f32[8,96,128]{2,1,0:T(8,128)}, f32[2,32,128]{2,1,0:T(8,128)}, f32[2,32,64]{2,1,0:T(8,128)}, f32[2,32,264]{2,1,0:T(8,128)}) custom-call(s32[16,1]{1,0:T(8,128)} %broadcast_subtract_fusion.rows_ref, s32[24,1]{1,0:T(8,128)} %copy.45.cols_ref, f32[4,8,64,128]{3,2,1,0:T(8,128)} %state.2, f32[4,8,1,66,264]{4,3,2,1,0:T(8,128)} %copy.46.top.bottom.state, ...), custom_call_target="tpu_custom_call" | custom-call | tf_op jit(solution)/shard_map/prepare/pallas_call | solution.py:432
  13.4 11.4 %edges.1 = (f32[8,96,128]{2,1,0:T(8,128)}, f32[2,32,128]{2,1,0:T(8,128)}, f32[2,32,64]{2,1,0:T(8,128)}, f32[2,32,264]{2,1,0:T(8,128)}) custom-call(f32[8,96,128]{2,1,0:T(8,128)} %get-tuple-element.24.refs_0_, f32[2,32,128]{2,1,0:T(8,128)} %get-tuple-element.25.refs_1_, f32[2,32,64]{2,1,0:T(8,128)} %get-tuple-element.26.refs_2_, ...), custom_call_target="tpu_custom_call" | custom-call | tf_op jit(solution)/shard_map/edges/pallas_call | solution.py:128
  24.9 0.1 copy.42
  25.0 0.1 reshape.56
  25.1 0.6 pad_add_fusion.meta
  25.6 2.2 %cycle.1.refs_0_ = f32[128,128]{1,0:T(8,128)} custom-call(s32[18]{0:T(128)} %pad_add_fusion.meta, f32[8,96,128]{2,1,0:T(8,128)} %get-tuple-element.31.got), custom_call_target="tpu_custom_call" | custom-call | tf_op jit(solution)/shard_map/cycle/pallas_call | solution.py:463
  27.8 10.7 %members.1.gath = f32[4,128,128]{2,1,0:T(8,128)} custom-call(f32[128,128]{1,0:T(8,128)} %cycle.1.refs_0_), custom_call_target="tpu_custom_call" | custom-call | tf_op jit(solution)/shard_map/members/pallas_call | solution.py:128
  38.5 0.0 copy-done.1
  38.6 2.1 %copy.49.old = f32[4,8,1,66,264]{4,3,2,1,0:T(8,128)} copy(f32[4,8,1,66,264]{4,2,3,1,0:T(1,128)S(1)} %copy-done.1) | data formatting | bytes 4460544 | tf_op args[3]
  40.6 12.3 %fine.1 = (f32[4,8,1,66,264]{4,3,2,1,0:T(8,128)}, f32[4,176,128]{2,1,0:T(8,128)}, f32[8,128]{1,0:T(8,128)}) custom-call(s32[18]{0:T(128)} %pad_add_fusion.meta, f32[4,4]{1,0:T(4,128)} %coupling.3, f32[4,128,128]{2,1,0:T(8,128)} %members.1.gath, f32[2,32,264]{2,1,0:T(8,128)} %get-tuple-element.32.halo, f32[4,8,1,66,264]{4,3,2,1,0:T(8,128)} %copy.46.top.bottom.state, ...), custom_call_target="tpu_custom_call" | custom-call | tf_op jit(solution)/shard_map/fine/pallas_call | solution.py:475
  52.9 7.0 %base.3 = (f32[4,8,64,128]{3,2,1,0:T(8,128)}, f32[8,128]{1,0:T(8,128)}) custom-call(s32[18]{0:T(128)} %pad_add_fusion.meta, f32[4,4]{1,0:T(4,128)} %coupling.3, f32[2,32,128]{2,1,0:T(8,128)} %get-tuple-element.28.rows, f32[2,32,64]{2,1,0:T(8,128)} %get-tuple-element.29.cols, f32[4,8,64,128]{3,2,1,0:T(8,128)} %state.2, f32[4,8,64,128]{3,2,1,0:T(8,128)} %old.2), custom_call_target="tpu_custom_call" | custom-call | tf_op jit(solution)/shard_map/base/pallas_call | solution.py:504
  59.9 1.3 add.20.refs_1_
  61.2 54.9 %owners.1 = (f32[8,4,176,128]{3,2,1,0:T(8,128)}, f32[8,8,128]{2,1,0:T(8,128)}) custom-call(f32[4,176,128]{2,1,0:T(8,128)} %get-tuple-element.33.refs_0_, f32[8,128]{1,0:T(8,128)} %add.20.refs_1_), custom_call_target="tpu_custom_call" | custom-call | tf_op jit(solution)/shard_map/owners/pallas_call | solution.py:128
  116.0 0.0 copy-start
  116.0 3.4 %sort.1 = (f32[4,4,176,128]{3,2,1,0:T(8,128)}, f32[8,128]{1,0:T(8,128)}) custom-call(s32[18]{0:T(128)} %pad_add_fusion.meta, f32[8,4,176,128]{3,2,1,0:T(8,128)} %get-tuple-element.36.got, f32[8,8,128]{2,1,0:T(8,128)} %get-tuple-element.37.sums), custom_call_target="tpu_custom_call" | custom-call | tf_op jit(solution)/shard_map/sort/pallas_call | solution.py:527
  119.5 22.4 %columns.1 = (f32[4,4,176,128]{3,2,1,0:T(8,128)}, f32[4,8,128]{2,1,0:T(8,128)}) custom-call(f32[4,4,176,128]{3,2,1,0:T(8,128)} %get-tuple-element.38.refs_0_, f32[8,128]{1,0:T(8,128)} %get-tuple-element.39.refs_1_), custom_call_target="tpu_custom_call" | custom-call | tf_op jit(solution)/shard_map/columns/pallas_call | solution.py:128
  141.9 4.2 %place.1 = (f32[4,8,64,128]{3,2,1,0:T(8,128)}, f32[1,1]{1,0:T(1,128)}) custom-call(s32[18]{0:T(128)} %pad_add_fusion.meta, f32[4,8,64,128]{3,2,1,0:T(8,128)} %get-tuple-element.30.tend, f32[4,4,176,128]{3,2,1,0:T(8,128)} %get-tuple-element.40.got, f32[4,8,128]{2,1,0:T(8,128)} %get-tuple-element.41.sums), custom_call_target="tpu_custom_call" | custom-call | tf_op jit(solution)/shard_map/place/pallas_call | solution.py:538
  146.1 0.0 copy-done
  146.1 5.0 %copy.50 = f32[4,8,1,66,264]{4,2,3,1,0:T(1,128)} copy(f32[4,8,1,66,264]{4,3,2,1,0:T(8,128)S(1)} %copy-done) | data formatting | bytes 4460544
  (1 shorter events, 0.0 us)
Async XLA Ops:
  8.4 30.2 %copy-start.1 = (f32[4,8,1,66,264]{4,2,3,1,0:T(1,128)S(1)}, f32[4,8,1,66,264]{4,2,3,1,0:T(1,128)}, u32[]{:S(2)}) copy-start(f32[4,8,1,66,264]{4,2,3,1,0:T(1,128)} %param.11) | copy-start | bytes 6690820
  116.0 30.0 %copy-start = (f32[4,8,1,66,264]{4,3,2,1,0:T(8,128)S(1)}, f32[4,8,1,66,264]{4,3,2,1,0:T(8,128)}, u32[]{:S(2)}) copy-start(f32[4,8,1,66,264]{4,3,2,1,0:T(8,128)} %get-tuple-element.58) | copy-start | bytes 6690820

commit v2 on v1

--- a/solution.py
+++ b/solution.py
@@ -140,10 +140,30 @@
     )(*arrays)
 
 
-def prepare_kernel(groups, last_row, rows_ref, cols_ref, base, top, bottom, cyc, brow, bcol, frow):
+def prepare_kernel(groups, offsets, owners, base, top, bottom, cyc, brow, bcol, frow, meta):
     fields, levels, block_x, block_y = base.shape
-    pick_rows = (iota((2 * groups, block_x), 1) == rows_ref[...]).astype(F32)
-    pick_cols = (iota((2 * groups + 8, block_y), 1) == cols_ref[...]).astype(F32)
+    row_block = lax.axis_index("gx")
+    col_block = lax.axis_index("gy")
+    meta[2 * groups] = row_block
+    meta[2 * groups + 1] = col_block
+    row_pick = jnp.full((2 * groups, block_x), -1, jnp.int32)
+    col_pick = jnp.full((2 * groups + 8, block_y), -1, jnp.int32)
+    row_slot = iota(row_pick.shape, 0)
+    col_slot = iota(col_pick.shape, 0)
+    for p in range(groups):
+        g = owners[p]
+        meta[2 * g] = offsets[p, 0]
+        meta[2 * g + 1] = offsets[p, 1]
+        row = offsets[p, 0] - row_block * block_x
+        col = offsets[p, 1] - col_block * block_y
+        row_pick = jnp.where(row_slot == g, row - 1, row_pick)
+        row_pick = jnp.where(row_slot == g + groups, row + PC, row_pick)
+        col_pick = jnp.where(col_slot == g, col - 1, col_pick)
+        col_pick = jnp.where(col_slot == g + groups, col + PC, col_pick)
+    col_pick = jnp.where(col_slot == 2 * groups, 0, col_pick)
+    col_pick = jnp.where(col_slot == 2 * groups + 1, block_y - 1, col_pick)
+    pick_rows = (iota(row_pick.shape, 1) == row_pick).astype(F32)
+    pick_cols = (iota(col_pick.shape, 1) == col_pick).astype(F32)
     for z in range(levels):
         for f in range(fields):
             q = base[f, z]
@@ -163,8 +183,8 @@
             brow[1, flat : flat + 1] = q[block_x - 1 :]
             bcol[0, flat : flat + 1] = side[2 * groups : 2 * groups + 1]
             bcol[1, flat : flat + 1] = side[2 * groups + 1 : 2 * groups + 2]
-            frow[0, flat : flat + 1] = top[f, z, 0, :1]
-            frow[1, flat : flat + 1] = bottom[f, z, 0, last_row : last_row + 1]
+            frow[0, flat : flat + 1] = top[f, z, 0]
+            frow[1, flat : flat + 1] = bottom[f, z, 0]
 
 
 def cycle_kernel(groups, fields, block_x, meta, got, piece):
@@ -238,7 +258,7 @@
 ):
     z = pl.program_id(0)
     fields, levels = state.shape[:2]
-    fine_rows, fine_cols = state.shape[3:]
+    fine_rows, fine_cols = state.shape[2], state.shape[4]
     piece = fine_rows // RATIO
     block_y = gath.shape[2]
     row_block = meta[2 * groups]
@@ -278,14 +298,14 @@
         right.append(turned[:fine_rows, fields + f : fields + f + 1])
 
     def cell(f, at):
-        return levels if f is None else state[f, at, 0]
+        return levels if f is None else state[f, at, :, 0, :]
 
     got = level(
-        cell, lambda f: old[f, 0, 0], coupling, z, first, last, left, right, float(RATIO)
+        cell, lambda f: old[f, 0, :, 0, :], coupling, z, first, last, left, right, float(RATIO)
     )
     squares = None
     for f in range(fields):
-        res[f, 0, 0] = got[f]
+        res[f, 0, :, 0, :] = got[f]
         squares = got[f] * got[f] if f == 0 else squares + got[f] * got[f]
         major = got[f].astype(BF16)
         minor = (got[f] - major.astype(F32)).astype(BF16)
@@ -411,44 +431,36 @@
 
 def local(sizes, base_state, base_old, fine_state, fine_old, coupling, patch_offsets, patch_group):
     groups, members = sizes["gx"], sizes["gy"]
-    row_block = lax.axis_index("gx")
-    col_block = lax.axis_index("gy")
     fields, levels, block_x, block_y = base_state.shape
     fine_rows, fine_cols = fine_state.shape[3:]
     piece = fine_rows // RATIO
     flat = fields * levels
-    owner = (patch_group[None, :] == jnp.arange(groups, dtype=jnp.int32)[:, None]).astype(jnp.int32)
-    placed = jnp.sum(owner[:, :, None] * patch_offsets[None, :, :], axis=1)
-    meta = jnp.concatenate([placed.reshape(-1), jnp.stack([row_block, col_block])])
-    row_pick = jnp.concatenate([placed[:, 0] - 1, placed[:, 0] + PC]) - row_block * block_x
-    col_pick = jnp.concatenate([placed[:, 1] - 1, placed[:, 1] + PC]) - col_block * block_y
-    ends = jnp.array([0, block_y - 1, -1, -1, -1, -1, -1, -1], jnp.int32)
-    col_pick = jnp.concatenate([col_pick, ends])
-
     def shape(*dims):
         return jax.ShapeDtypeStruct(dims, F32)
 
     tail = fine_rows - 1
-    cyc, brow, bcol, frow = pl.pallas_call(
-        functools.partial(prepare_kernel, groups, tail % 8),
+    fine_turned = jnp.swapaxes(fine_state, 2, 3)
+    cyc, brow, bcol, frow, meta = pl.pallas_call(
+        functools.partial(prepare_kernel, groups),
         grid=(1,),
         out_shape=[
             shape(groups, 3 * flat, block_y),
             shape(2, flat, block_y),
             shape(2, flat, block_x),
             shape(2, flat, fine_cols),
+            jax.ShapeDtypeStruct((2 * groups + 2,), jnp.int32),
         ],
         in_specs=[
+            SMEM,
+            SMEM,
             VMEM,
-            VMEM,
-            VMEM,
-            pl.BlockSpec((fields, levels, 1, 8, fine_cols), lambda i: (0, 0, 0, 0, 0)),
-            pl.BlockSpec((fields, levels, 1, 8, fine_cols), lambda i: (0, 0, 0, tail // 8, 0)),
-        ],
-        out_specs=[VMEM] * 4,
+            pl.BlockSpec((fields, levels, 1, 1, fine_cols), lambda i: (0, 0, 0, 0, 0)),
+            pl.BlockSpec((fields, levels, 1, 1, fine_cols), lambda i: (0, 0, tail, 0, 0)),
+        ],
+        out_specs=[VMEM] * 4 + [SMEM],
         compiler_params=params(),
         name="prepare",
-    )(row_pick[:, None], col_pick[:, None], base_state, fine_state, fine_state)
+    )(patch_offsets, patch_group, base_state, fine_turned, fine_turned)
 
     cyc, brow, bcol, frow = communicate(
         "edges",
@@ -470,8 +482,8 @@
     )(meta, cyc)
     (gath,) = communicate("members", 2, sizes, (("gather", "gy"),), cycle)
 
-    slab = (fields, levels, 1, fine_rows, fine_cols)
-    thin = (fields, 1, 1, fine_rows, fine_cols)
+    slab = (fields, levels, fine_rows, 1, fine_cols)
+    thin = (fields, 1, fine_rows, 1, fine_cols)
     fine_res, rest, fine_sq = pl.pallas_call(
         functools.partial(fine_kernel, groups, members),
         grid=(levels,),
@@ -497,7 +509,7 @@
         ],
         compiler_params=params(),
         name="fine",
-    )(meta, coupling, gath, frow, fine_state, fine_old)
+    )(meta, coupling, gath, frow, fine_turned, jnp.swapaxes(fine_old, 2, 3))
 
     whole = (fields, levels, block_x, block_y)
     sheet = (fields, 1, block_x, block_y)
@@ -544,7 +556,7 @@
         compiler_params=params(),
         name="place",
     )(meta, tend, slots, sums)
-    return (base_out, fine_res, norm[0, 0])
+    return (base_out, jnp.swapaxes(fine_res, 2, 3), norm[0, 0])
 
 
 def solution(mesh):

time: 151 us -> 144 us (0.954); the launches traced: 151 us -> 142 us
  local copies, waits for them, and re-layouts: 12 us -> 1.35 us
  Pallas kernels: 134 us -> 139 us
  other arithmetic: 4.84 us -> 1.28 us
    unnamed x7 -> x3, local copies, waits for them, and re-layouts: 11.1 us -> 1.35 us
    pallas_call x1, Pallas kernels: 12.3 us -> 19.2 us  [local(): pl.pallas_call(functools.partial(fine_kernel, groups, members), grid=(lev...]
where the time goes in v2:
time: 144 us; the launch traced here: 142 us
  Pallas kernels  139 us (97%)
    pallas_call x4, Pallas kernels, communicate(): pl.pallas_call(functools.partial(comm_kernel, plan, axes, inner), out_sha...  99.4 us
    pallas_call x1, Pallas kernels, local(): pl.pallas_call(functools.partial(fine_kernel, groups, members), grid=(lev...  19.2 us
    pallas_call x1, Pallas kernels, local(): pl.pallas_call(functools.partial(base_kernel, groups, members), grid=(lev...  6.99 us
    pallas_call x1, Pallas kernels, local(): pl.pallas_call(functools.partial(prepare_kernel, groups), grid=(1,), out_...  4.72 us
    pallas_call x1, Pallas kernels, local(): pl.pallas_call(functools.partial(sort_kernel, groups, members, block_x),...  3.33 us
    pallas_call x1, Pallas kernels, local(): pl.pallas_call(functools.partial(place_kernel, groups, members), out_shap...  3.16 us

profile of v2, /device:TPU:29, one launch (start us, length us, event | category | flops | bytes accessed | tf_op | source)
XLA Modules:
  0.0 142.3 jit_solution(9816327240494398328)
XLA Ops:
  0.6 1.3 copy.10.offsets
  2.0 4.7 %prepare.1 = (f32[8,96,128]{2,1,0:T(8,128)}, f32[2,32,128]{2,1,0:T(8,128)}, f32[2,32,64]{2,1,0:T(8,128)}, f32[2,32,264]{2,1,0:T(8,128)}, s32[18]{0:T(128)}) custom-call(s32[8,2]{1,0:T(8,128)} %copy.10.offsets, s32[8]{0:T(128)} %owners.2, f32[4,8,64,128]{3,2,1,0:T(8,128)} %state.1, f32[4,8,66,1,264]{4,3,2,1,0:T(1,128)} %bitcast.4, f32[4,8,66,1,264]{4,3,2,1,0:T(1,128)} %bitcast.5), custom_call_target="tpu_custom_call" | custom-call | tf_op jit(solution)/shard_map/prepare/pallas_call | solution.py:443
  6.7 11.5 %edges.1 = (f32[8,96,128]{2,1,0:T(8,128)}, f32[2,32,128]{2,1,0:T(8,128)}, f32[2,32,64]{2,1,0:T(8,128)}, f32[2,32,264]{2,1,0:T(8,128)}) custom-call(f32[8,96,128]{2,1,0:T(8,128)} %get-tuple-element.26.refs_0_, f32[2,32,128]{2,1,0:T(8,128)} %get-tuple-element.27.refs_1_, f32[2,32,64]{2,1,0:T(8,128)} %get-tuple-element.28.refs_2_, ...), custom_call_target="tpu_custom_call" | custom-call | tf_op jit(solution)/shard_map/edges/pallas_call | solution.py:128
  18.2 2.2 %cycle.1.refs_0_ = f32[128,128]{1,0:T(8,128)} custom-call(s32[18]{0:T(128)} %get-tuple-element.25.meta, f32[8,96,128]{2,1,0:T(8,128)} %get-tuple-element.33.got), custom_call_target="tpu_custom_call" | custom-call | tf_op jit(solution)/shard_map/cycle/pallas_call | solution.py:475
  20.4 10.7 %members.1.gath = f32[4,128,128]{2,1,0:T(8,128)} custom-call(f32[128,128]{1,0:T(8,128)} %cycle.1.refs_0_), custom_call_target="tpu_custom_call" | custom-call | tf_op jit(solution)/shard_map/members/pallas_call | solution.py:128
  31.1 7.0 %base.3 = (f32[4,8,64,128]{3,2,1,0:T(8,128)}, f32[8,128]{1,0:T(8,128)}) custom-call(s32[18]{0:T(128)} %get-tuple-element.25.meta, f32[4,4]{1,0:T(4,128)} %coupling.3, f32[2,32,128]{2,1,0:T(8,128)} %get-tuple-element.30.rows, f32[2,32,64]{2,1,0:T(8,128)} %get-tuple-element.31.cols, f32[4,8,64,128]{3,2,1,0:T(8,128)} %state.1, f32[4,8,64,128]{3,2,1,0:T(8,128)} %old.1), custom_call_target="tpu_custom_call" | custom-call | tf_op jit(solution)/shard_map/base/pallas_call | solution.py:516
  38.0 0.0 copy-start
  38.0 19.2 %fine.1 = (f32[4,8,66,1,264]{4,3,2,1,0:T(1,128)}, f32[4,176,128]{2,1,0:T(8,128)}, f32[8,128]{1,0:T(8,128)}) custom-call(s32[18]{0:T(128)} %get-tuple-element.25.meta, f32[4,4]{1,0:T(4,128)} %coupling.3, f32[4,128,128]{2,1,0:T(8,128)} %members.1.gath, f32[2,32,264]{2,1,0:T(8,128)} %get-tuple-element.34.halo, f32[4,8,66,1,264]{4,3,2,1,0:T(1,128)} %bitcast.6, ...), custom_call_target="tpu_custom_call" | custom-call | tf_op jit(solution)/shard_map/fine/pallas_call | solution.py:487
  57.2 0.0 copy-done
  57.2 1.3 add.3.refs_1_
  58.5 54.9 %owners.3 = (f32[8,4,176,128]{3,2,1,0:T(8,128)}, f32[8,8,128]{2,1,0:T(8,128)}) custom-call(f32[4,176,128]{2,1,0:T(8,128)} %get-tuple-element.35.refs_0_, f32[8,128]{1,0:T(8,128)} %add.3.refs_1_), custom_call_target="tpu_custom_call" | custom-call | tf_op jit(solution)/shard_map/owners/pallas_call | solution.py:128
  113.4 3.3 %sort.1 = (f32[4,4,176,128]{3,2,1,0:T(8,128)}, f32[8,128]{1,0:T(8,128)}) custom-call(s32[18]{0:T(128)} %get-tuple-element.25.meta, f32[8,4,176,128]{3,2,1,0:T(8,128)} %get-tuple-element.38.got, f32[8,8,128]{2,1,0:T(8,128)} %get-tuple-element.39.sums), custom_call_target="tpu_custom_call" | custom-call | tf_op jit(solution)/shard_map/sort/pallas_call | solution.py:539
  116.7 22.4 %columns.1 = (f32[4,4,176,128]{3,2,1,0:T(8,128)}, f32[4,8,128]{2,1,0:T(8,128)}) custom-call(f32[4,4,176,128]{3,2,1,0:T(8,128)} %get-tuple-element.40.refs_0_, f32[8,128]{1,0:T(8,128)} %get-tuple-element.41.refs_1_), custom_call_target="tpu_custom_call" | custom-call | tf_op jit(solution)/shard_map/columns/pallas_call | solution.py:128
  139.1 3.2 %place.1 = (f32[4,8,64,128]{3,2,1,0:T(8,128)}, f32[1,1]{1,0:T(1,128)}) custom-call(s32[18]{0:T(128)} %get-tuple-element.25.meta, f32[4,8,64,128]{3,2,1,0:T(8,128)} %get-tuple-element.32.tend, f32[4,4,176,128]{3,2,1,0:T(8,128)} %get-tuple-element.42.got, f32[4,8,128]{2,1,0:T(8,128)} %get-tuple-element.43.sums), custom_call_target="tpu_custom_call" | custom-call | tf_op jit(solution)/shard_map/place/pallas_call | solution.py:550
Async XLA Ops:
  38.0 19.2 %copy-start = (f32[8,128]{1,0:T(8,128)S(1)}, f32[8,128]{1,0:T(8,128)}, u32[]{:S(2)}) copy-start(f32[8,128]{1,0:T(8,128)} %get-tuple-element.37) | copy-start | bytes 12292

commit v3 on v2

--- a/solution.py
+++ b/solution.py
@@ -78,29 +78,14 @@
         own.start()
         local.append(own)
         if mode == "relay":
-            outer = size // inner
-            high, low = lax.div(me, inner), lax.rem(me, inner)
-            for step in range(1, outer):
-                peer = lax.rem(high + step, outer) * inner + low
-                origin = lax.rem(high + outer - step, outer) * inner + low
-                relays.append((send(source, target.at[me], axis, peer), target, origin))
-            for hop in range(1, inner):
-                peer = high * inner + lax.rem(low + hop, inner)
-                waiting.append(send(source, target.at[me], axis, peer))
+            relays.append((source, target, axis))
             continue
         for step in range(1, size):
             peer = lax.rem(me + step, size)
             part = source.at[peer] if mode == "exchange" else source
             waiting.append(send(part, target.at[me], axis, peer))
-    for copy, target, origin in relays:
-        copy.wait_recv()
-        me = lax.axis_index("gx")
-        high, low = lax.div(me, inner), lax.rem(me, inner)
-        for hop in range(1, inner):
-            peer = high * inner + lax.rem(low + hop, inner)
-            waiting.append(send(target.at[origin], target.at[origin], "gx", peer))
-    for copy, _, _ in relays:
-        copy.wait_send()
+    for source, target, axis in relays:
+        relay(source, target, axis, axes[axis], inner, send_sem, recv_sem, used[0])
     for copy in waiting:
         copy.wait()
     for copy in local:
@@ -123,7 +108,7 @@
             slots += size - 1
             shapes.append(array.shape)
         else:
-            slots += size - 1
+            slots += len(relay_slots(array.shape[0], size, inner)) if mode == "relay" else size - 1
             shapes.append((size, *array.shape))
     return pl.pallas_call(
         functools.partial(comm_kernel, plan, axes, inner),
@@ -138,6 +123,102 @@
         compiler_params=params(collective_id=ident, has_side_effects=True),
         name=name,
     )(*arrays)
+
+
+def relay_slots(fields, size, inner):
+    outer = size // inner
+    keys = [("own", f, 0, hop) for f in range(fields) for hop in range(1, inner)]
+    for f in range(fields):
+        if f < fields // 2:
+            for way in ("up", "down"):
+                keys += [(way, f, 0, d) for d in range(1, outer)]
+                keys += [
+                    (way + "x", f, hop, d) for d in range(1, outer) for hop in range(1, inner)
+                ]
+        else:
+            for way in ("up", "down"):
+                keys += [(way, f, hop, d) for d in range(1, outer) for hop in range(inner)]
+    return {key: slot for slot, key in enumerate(keys)}
+
+
+def relay(source, target, axis, size, inner, send_sem, recv_sem, base):
+    fields = source.shape[0]
+    outer = size // inner
+    me = lax.axis_index(axis)
+    high, low = lax.div(me, inner), lax.rem(me, inner)
+    slots = relay_slots(fields, size, inner)
+    has_up, has_down = high < outer - 1, high > 0
+    early, late = range(fields // 2), range(fields // 2, fields)
+
+    def place(step, hop):
+        return (high - step) * inner + lax.rem(low + inner - hop, inner)
+
+    def across(hop):
+        return high * inner + lax.rem(low + hop, inner)
+
+    def copy(key, origin, peer, own=False):
+        return pltpu.make_async_remote_copy(
+            src_ref=source.at[key[1]] if own else target.at[origin, key[1]],
+            dst_ref=target.at[origin, key[1]],
+            send_sem=send_sem.at[base + slots[key]],
+            recv_sem=recv_sem.at[base + slots[key]],
+            device_id={axis: peer},
+            device_id_type=MESH,
+        )
+
+    finish = []
+
+    def start(key, origin, peer, own, *conditions):
+        ready = conditions[0] if conditions else None
+        for more in conditions[1:]:
+            ready = ready & more
+        made = copy(key, origin, peer, own)
+        if ready is None:
+            made.start()
+        else:
+            pl.when(ready)(made.start)
+        finish.append((made, ready))
+
+    for f in (*late, *early):
+        for hop in range(1, inner):
+            start(("own", f, 0, hop), me, across(hop), True)
+        start(("up", f, 0, 1), me, me + inner, True, has_up)
+        start(("down", f, 0, 1), me, me - inner, True, has_down)
+    for f in late:
+        for hop in range(1, inner):
+            origin = place(0, hop)
+            copy(("own", f, 0, hop), origin, me).wait_recv()
+            start(("up", f, hop, 1), origin, me + inner, False, has_up)
+            start(("down", f, hop, 1), origin, me - inner, False, has_down)
+    for d in range(1, outer):
+        for f in range(fields):
+            for hop in range(1 if f in early else inner):
+                for way, sign, exists, onward in (
+                    ("up", 1, high >= d, has_up),
+                    ("down", -1, high + d < outer, has_down),
+                ):
+                    origin = place(sign * d, hop)
+                    pl.when(exists)(copy((way, f, hop, d), origin, me).wait_recv)
+                    if d + 1 < outer:
+                        start(
+                            (way, f, hop, d + 1), origin, me + sign * inner, False, exists, onward
+                        )
+                    if f in early:
+                        for jump in range(1, inner):
+                            start((way + "x", f, jump, d), origin, across(jump), False, exists)
+    for f in early:
+        for hop in range(1, inner):
+            copy(("own", f, 0, hop), place(0, hop), me).wait_recv()
+            for d in range(1, outer):
+                got = copy(("upx", f, hop, d), place(d, hop), me)
+                pl.when(high >= d)(got.wait_recv)
+                got = copy(("downx", f, hop, d), place(-d, hop), me)
+                pl.when(high + d < outer)(got.wait_recv)
+    for made, ready in finish:
+        if ready is None:
+            made.wait_send()
+        else:
+            pl.when(ready)(made.wait_send)
 
 
 def prepare_kernel(groups, offsets, owners, base, top, bottom, cyc, brow, bcol, frow, meta):
@@ -254,7 +335,7 @@
 
 
 def fine_kernel(
-    groups, members, meta, coupling, gath, halo, state, old, res, rest, sq, edge, side, fit, thin
+    groups, members, meta, coupling, gath, halo, state, old, res, rest, sq, edge, side, fit, thin, ring
 ):
     z = pl.program_id(0)
     fields, levels = state.shape[:2]
@@ -285,6 +366,14 @@
         cell = iota((fine_cols, 128), 0) // RATIO + start_y
         fit[...] = (lax.rem(cell, block_y) == iota((fine_cols, 128), 1)).astype(F32).astype(BF16)
 
+        for f in range(fields):
+            ring[0, f] = state[f, 0, :, 0, :]
+
+    @pl.when(z + 1 < levels)
+    def _():
+        for f in range(fields):
+            ring[lax.rem(z + 1, 3), f] = state[f, z + 1, :, 0, :]
+
     at = pl.multiple_of(z * 2 * fields, 8)
     edges = edge[pl.ds(at, 2 * fields)]
     turned = jnp.transpose(side[pl.ds(at, 2 * fields)])
@@ -298,7 +387,7 @@
         right.append(turned[:fine_rows, fields + f : fields + f + 1])
 
     def cell(f, at):
-        return levels if f is None else state[f, at, :, 0, :]
+        return levels if f is None else ring[lax.rem(at, 3), f]
 
     got = level(
         cell, lambda f: old[f, 0, :, 0, :], coupling, z, first, last, left, right, float(RATIO)
@@ -506,6 +595,7 @@
             pltpu.VMEM((2 * flat, 128), F32),
             pltpu.VMEM((fine_cols, 128), BF16),
             pltpu.VMEM((fields, fine_rows, 128), F32),
+            pltpu.VMEM((3, fields, fine_rows, fine_cols), F32),
         ],
         compiler_params=params(),
         name="fine",

time: 144 us -> 128 us (0.89)
  the two profiles are of different devices: /device:TPU:29 before, /device:TPU:0 now
where the time goes in v3:
time: 128 us; the launch traced here: 127 us
  Pallas kernels  124 us (97%)
  local copies, waits for them, and re-layouts  1.35 us (1%)
  other arithmetic  1.28 us (1%)
    pallas_call x4, Pallas kernels, communicate(): pl.pallas_call(functools.partial(comm_kernel, plan, axes, inner), out_sha...  90.1 us
    pallas_call x1, Pallas kernels, local(): pl.pallas_call(functools.partial(fine_kernel, groups, members), grid=(lev...  13.2 us
    pallas_call x1, Pallas kernels, local(): pl.pallas_call(functools.partial(base_kernel, groups, members), grid=(lev...  6.99 us
    pallas_call x1, Pallas kernels, local(): pl.pallas_call(functools.partial(prepare_kernel, groups), grid=(1,), out_...  4.72 us
    pallas_call x1, Pallas kernels, local(): pl.pallas_call(functools.partial(sort_kernel, groups, members, block_x),...  3.26 us
    pallas_call x1, Pallas kernels, local(): pl.pallas_call(functools.partial(place_kernel, groups, members), out_shap...  3.16 us

profile of v3, /device:TPU:0, one launch (start us, length us, event | category | flops | bytes accessed | tf_op | source)
XLA Modules:
  0.0 126.9 jit_solution(1757800661886913034)
XLA Ops:
  0.6 1.3 %copy.10.offsets = s32[8,2]{1,0:T(8,128)} copy(s32[8,2]{0,1:T(2,128)} %param.12) | data formatting | bytes 128 | tf_op args[5]
  2.0 4.7 %prepare.1 = (f32[8,96,128]{2,1,0:T(8,128)}, f32[2,32,128]{2,1,0:T(8,128)}, f32[2,32,64]{2,1,0:T(8,128)}, f32[2,32,264]{2,1,0:T(8,128)}, s32[18]{0:T(128)}) custom-call(s32[8,2]{1,0:T(8,128)} %copy.10.offsets, s32[8]{0:T(128)} %owners.2, f32[4,8,64,128]{3,2,1,0:T(8,128)} %state.1, f32[4,8,66,1,264]{4,3,2,1,0:T(1,128)} %bitcast.4, f32[4,8,66,1,264]{4,3,2,1,0:T(1,128)} %bitcast.5), custom_call_target="tpu_custom_call" | custom-call | tf_op jit(solution)/shard_map/prepare/pallas_call | solution.py:532
  6.7 17.5 %edges.1 = (f32[8,96,128]{2,1,0:T(8,128)}, f32[2,32,128]{2,1,0:T(8,128)}, f32[2,32,64]{2,1,0:T(8,128)}, f32[2,32,264]{2,1,0:T(8,128)}) custom-call(f32[8,96,128]{2,1,0:T(8,128)} %get-tuple-element.26.refs_0_, f32[2,32,128]{2,1,0:T(8,128)} %get-tuple-element.27.refs_1_, f32[2,32,64]{2,1,0:T(8,128)} %get-tuple-element.28.refs_2_, ...), custom_call_target="tpu_custom_call" | custom-call | tf_op jit(solution)/shard_map/edges/pallas_call | solution.py:113
  24.2 2.2 %cycle.1.refs_0_ = f32[128,128]{1,0:T(8,128)} custom-call(s32[18]{0:T(128)} %get-tuple-element.25.meta, f32[8,96,128]{2,1,0:T(8,128)} %get-tuple-element.33.got), custom_call_target="tpu_custom_call" | custom-call | tf_op jit(solution)/shard_map/cycle/pallas_call | solution.py:564
  26.4 6.6 %members.1.gath = f32[4,128,128]{2,1,0:T(8,128)} custom-call(f32[128,128]{1,0:T(8,128)} %cycle.1.refs_0_), custom_call_target="tpu_custom_call" | custom-call | tf_op jit(solution)/shard_map/members/pallas_call | solution.py:113
  33.0 7.0 %base.3 = (f32[4,8,64,128]{3,2,1,0:T(8,128)}, f32[8,128]{1,0:T(8,128)}) custom-call(s32[18]{0:T(128)} %get-tuple-element.25.meta, f32[4,4]{1,0:T(4,128)} %coupling.3, f32[2,32,128]{2,1,0:T(8,128)} %get-tuple-element.30.rows, f32[2,32,64]{2,1,0:T(8,128)} %get-tuple-element.31.cols, f32[4,8,64,128]{3,2,1,0:T(8,128)} %state.1, f32[4,8,64,128]{3,2,1,0:T(8,128)} %old.1), custom_call_target="tpu_custom_call" | custom-call | tf_op jit(solution)/shard_map/base/pallas_call | solution.py:606
  40.0 0.0 copy-start
  40.0 13.2 %fine.1 = (f32[4,8,66,1,264]{4,3,2,1,0:T(1,128)}, f32[4,176,128]{2,1,0:T(8,128)}, f32[8,128]{1,0:T(8,128)}) custom-call(s32[18]{0:T(128)} %get-tuple-element.25.meta, f32[4,4]{1,0:T(4,128)} %coupling.3, f32[4,128,128]{2,1,0:T(8,128)} %members.1.gath, f32[2,32,264]{2,1,0:T(8,128)} %get-tuple-element.34.halo, f32[4,8,66,1,264]{4,3,2,1,0:T(1,128)} %bitcast.6, ...), custom_call_target="tpu_custom_call" | custom-call | tf_op jit(solution)/shard_map/fine/pallas_call | solution.py:576
  53.2 0.0 copy-done
  53.2 1.3 %add.3.refs_1_ = f32[8,128]{1,0:T(8,128)} add(f32[8,128]{1,0:T(8,128)} %get-tuple-element.36, f32[8,128]{1,0:T(8,128)S(1)} %copy-done) | non-fusion elementwise | flops 1024 | bytes 12288 | tf_op jit(solution)/shard_map/add | solution.py:627
  54.5 44.7 %owners.3 = (f32[8,4,176,128]{3,2,1,0:T(8,128)}, f32[8,8,128]{2,1,0:T(8,128)}) custom-call(f32[4,176,128]{2,1,0:T(8,128)} %get-tuple-element.35.refs_0_, f32[8,128]{1,0:T(8,128)} %add.3.refs_1_), custom_call_target="tpu_custom_call" | custom-call | tf_op jit(solution)/shard_map/owners/pallas_call | solution.py:113
  99.2 3.3 %sort.1 = (f32[4,4,176,128]{3,2,1,0:T(8,128)}, f32[8,128]{1,0:T(8,128)}) custom-call(s32[18]{0:T(128)} %get-tuple-element.25.meta, f32[8,4,176,128]{3,2,1,0:T(8,128)} %get-tuple-element.38.got, f32[8,8,128]{2,1,0:T(8,128)} %get-tuple-element.39.sums), custom_call_target="tpu_custom_call" | custom-call | tf_op jit(solution)/shard_map/sort/pallas_call | solution.py:629
  102.4 21.3 %columns.1 = (f32[4,4,176,128]{3,2,1,0:T(8,128)}, f32[4,8,128]{2,1,0:T(8,128)}) custom-call(f32[4,4,176,128]{3,2,1,0:T(8,128)} %get-tuple-element.40.refs_0_, f32[8,128]{1,0:T(8,128)} %get-tuple-element.41.refs_1_), custom_call_target="tpu_custom_call" | custom-call | tf_op jit(solution)/shard_map/columns/pallas_call | solution.py:113
  123.8 3.2 %place.1 = (f32[4,8,64,128]{3,2,1,0:T(8,128)}, f32[1,1]{1,0:T(1,128)}) custom-call(s32[18]{0:T(128)} %get-tuple-element.25.meta, f32[4,8,64,128]{3,2,1,0:T(8,128)} %get-tuple-element.32.tend, f32[4,4,176,128]{3,2,1,0:T(8,128)} %get-tuple-element.42.got, f32[4,8,128]{2,1,0:T(8,128)} %get-tuple-element.43.sums), custom_call_target="tpu_custom_call" | custom-call | tf_op jit(solution)/shard_map/place/pallas_call | solution.py:640
Async XLA Ops:
  40.0 13.2 %copy-start = (f32[8,128]{1,0:T(8,128)S(1)}, f32[8,128]{1,0:T(8,128)}, u32[]{:S(2)}) copy-start(f32[8,128]{1,0:T(8,128)} %get-tuple-element.37) | copy-start | bytes 12292

commit v4 on v3

--- a/solution.py
+++ b/solution.py
@@ -233,10 +233,10 @@
     col_slot = iota(col_pick.shape, 0)
     for p in range(groups):
         g = owners[p]
-        meta[2 * g] = offsets[p, 0]
-        meta[2 * g + 1] = offsets[p, 1]
-        row = offsets[p, 0] - row_block * block_x
-        col = offsets[p, 1] - col_block * block_y
+        meta[2 * g] = offsets[0, p]
+        meta[2 * g + 1] = offsets[1, p]
+        row = offsets[0, p] - row_block * block_x
+        col = offsets[1, p] - col_block * block_y
         row_pick = jnp.where(row_slot == g, row - 1, row_pick)
         row_pick = jnp.where(row_slot == g + groups, row + PC, row_pick)
         col_pick = jnp.where(col_slot == g, col - 1, col_pick)
@@ -335,7 +335,7 @@
 
 
 def fine_kernel(
-    groups, members, meta, coupling, gath, halo, state, old, res, rest, sq, edge, side, fit, thin, ring
+    groups, members, meta, coupling, gath, halo, sums, state, old, res, rest, sq, edge, side, fit, thin, ring
 ):
     z = pl.program_id(0)
     fields, levels = state.shape[:2]
@@ -349,7 +349,7 @@
 
     @pl.when(z == 0)
     def _():
-        sq[...] = jnp.zeros_like(sq)
+        sq[...] = sums[...]
         lane = iota((block_y, fine_cols), 0)
         fine = iota((block_y, fine_cols), 1) // RATIO
         rows = None
@@ -549,7 +549,7 @@
         out_specs=[VMEM] * 4 + [SMEM],
         compiler_params=params(),
         name="prepare",
-    )(patch_offsets, patch_group, base_state, fine_turned, fine_turned)
+    )(patch_offsets.T, patch_group, base_state, fine_turned, fine_turned)
 
     cyc, brow, bcol, frow = communicate(
         "edges",
@@ -571,36 +571,6 @@
     )(meta, cyc)
     (gath,) = communicate("members", 2, sizes, (("gather", "gy"),), cycle)
 
-    slab = (fields, levels, fine_rows, 1, fine_cols)
-    thin = (fields, 1, fine_rows, 1, fine_cols)
-    fine_res, rest, fine_sq = pl.pallas_call(
-        functools.partial(fine_kernel, groups, members),
-        grid=(levels,),
-        out_shape=[shape(*slab), shape(fields, piece * levels, 128), shape(8, 128)],
-        in_specs=[
-            SMEM,
-            SMEM,
-            VMEM,
-            VMEM,
-            pl.BlockSpec(slab, lambda z: (0, 0, 0, 0, 0)),
-            pl.BlockSpec(thin, lambda z: (0, z, 0, 0, 0)),
-        ],
-        out_specs=[
-            pl.BlockSpec(thin, lambda z: (0, z, 0, 0, 0)),
-            pl.BlockSpec((fields, piece * levels, 128), lambda z: (0, 0, 0)),
-            pl.BlockSpec((8, 128), lambda z: (0, 0)),
-        ],
-        scratch_shapes=[
-            pltpu.VMEM((2 * flat, fine_cols), F32),
-            pltpu.VMEM((2 * flat, 128), F32),
-            pltpu.VMEM((fine_cols, 128), BF16),
-            pltpu.VMEM((fields, fine_rows, 128), F32),
-            pltpu.VMEM((3, fields, fine_rows, fine_cols), F32),
-        ],
-        compiler_params=params(),
-        name="fine",
-    )(meta, coupling, gath, frow, fine_turned, jnp.swapaxes(fine_old, 2, 3))
-
     whole = (fields, levels, block_x, block_y)
     sheet = (fields, 1, block_x, block_y)
     tend, base_sq = pl.pallas_call(
@@ -623,8 +593,39 @@
         name="base",
     )(meta, coupling, brow, bcol, base_state, base_old)
 
+    slab = (fields, levels, fine_rows, 1, fine_cols)
+    thin = (fields, 1, fine_rows, 1, fine_cols)
+    fine_res, rest, fine_sq = pl.pallas_call(
+        functools.partial(fine_kernel, groups, members),
+        grid=(levels,),
+        out_shape=[shape(*slab), shape(fields, piece * levels, 128), shape(8, 128)],
+        in_specs=[
+            SMEM,
+            SMEM,
+            VMEM,
+            VMEM,
+            VMEM,
+            pl.BlockSpec(slab, lambda z: (0, 0, 0, 0, 0)),
+            pl.BlockSpec(thin, lambda z: (0, z, 0, 0, 0)),
+        ],
+        out_specs=[
+            pl.BlockSpec(thin, lambda z: (0, z, 0, 0, 0)),
+            pl.BlockSpec((fields, piece * levels, 128), lambda z: (0, 0, 0)),
+            pl.BlockSpec((8, 128), lambda z: (0, 0)),
+        ],
+        scratch_shapes=[
+            pltpu.VMEM((2 * flat, fine_cols), F32),
+            pltpu.VMEM((2 * flat, 128), F32),
+            pltpu.VMEM((fine_cols, 128), BF16),
+            pltpu.VMEM((fields, fine_rows, 128), F32),
+            pltpu.VMEM((3, fields, fine_rows, fine_cols), F32),
+        ],
+        compiler_params=params(),
+        name="fine",
+    )(meta, coupling, gath, frow, base_sq, fine_turned, jnp.swapaxes(fine_old, 2, 3))
+
     gathered, sums = communicate(
-        "owners", 3, sizes, (("relay", "gx"), ("gather", "gx")), rest, fine_sq + base_sq
+        "owners", 3, sizes, (("relay", "gx"), ("gather", "gx")), rest, fine_sq
     )
     slots, total = pl.pallas_call(
         functools.partial(sort_kernel, groups, members, block_x),

time: 128 us -> 125 us (0.977)
  local copies, waits for them, and re-layouts: 1.35 us -> 0 us
  other arithmetic: 1.28 us -> 0 us
    unnamed x3 -> x0, local copies, waits for them, and re-layouts: 1.35 us -> none
where the time goes in v4:
time: 125 us
  Pallas kernels  124 us (99%)
    pallas_call x4, Pallas kernels, communicate(): pl.pallas_call(functools.partial(comm_kernel, plan, axes, inner), out_sha...  90.1 us
    pallas_call x1, Pallas kernels, local(): pl.pallas_call(functools.partial(fine_kernel, groups, members), grid=(lev...  13.2 us
    pallas_call x1, Pallas kernels, local(): pl.pallas_call(functools.partial(base_kernel, groups, members), grid=(lev...  6.96 us
    pallas_call x1, Pallas kernels, local(): pl.pallas_call(functools.partial(prepare_kernel, groups), grid=(1,), out_...  4.73 us
    pallas_call x1, Pallas kernels, local(): pl.pallas_call(functools.partial(place_kernel, groups, members), out_shap...  3.73 us
    pallas_call x1, Pallas kernels, local(): pl.pallas_call(functools.partial(sort_kernel, groups, members, block_x),...  3.28 us

profile of v4, /device:TPU:0, one launch (start us, length us, event | category | flops | bytes accessed | tf_op | source)
XLA Modules:
  0.0 124.9 jit_solution(2522377876093609938)
XLA Ops:
  0.6 4.7 %prepare.1 = (f32[8,96,128]{2,1,0:T(8,128)}, f32[2,32,128]{2,1,0:T(8,128)}, f32[2,32,64]{2,1,0:T(8,128)}, f32[2,32,264]{2,1,0:T(8,128)}, s32[18]{0:T(128)}) custom-call(s32[2,8]{1,0:T(2,128)} %bitcast.9, s32[8]{0:T(128)} %owners.2, f32[4,8,64,128]{3,2,1,0:T(8,128)} %state.1, f32[4,8,66,1,264]{4,3,2,1,0:T(1,128)} %bitcast.5, f32[4,8,66,1,264]{4,3,2,1,0:T(1,128)} %bitcast.6), custom_call_target="tpu_custom_call" | custom-call | tf_op jit(solution)/shard_map/prepare/pallas_call | solution.py:532
  5.4 17.5 %edges.1 = (f32[8,96,128]{2,1,0:T(8,128)}, f32[2,32,128]{2,1,0:T(8,128)}, f32[2,32,64]{2,1,0:T(8,128)}, f32[2,32,264]{2,1,0:T(8,128)}) custom-call(f32[8,96,128]{2,1,0:T(8,128)} %get-tuple-element.26.refs_0_, f32[2,32,128]{2,1,0:T(8,128)} %get-tuple-element.27.refs_1_, f32[2,32,64]{2,1,0:T(8,128)} %get-tuple-element.28.refs_2_, ...), custom_call_target="tpu_custom_call" | custom-call | tf_op jit(solution)/shard_map/edges/pallas_call | solution.py:113
  22.9 2.2 %cycle.1.refs_0_ = f32[128,128]{1,0:T(8,128)} custom-call(s32[18]{0:T(128)} %get-tuple-element.25.meta, f32[8,96,128]{2,1,0:T(8,128)} %get-tuple-element.33.got), custom_call_target="tpu_custom_call" | custom-call | tf_op jit(solution)/shard_map/cycle/pallas_call | solution.py:564
  25.1 6.6 %members.1.gath = f32[4,128,128]{2,1,0:T(8,128)} custom-call(f32[128,128]{1,0:T(8,128)} %cycle.1.refs_0_), custom_call_target="tpu_custom_call" | custom-call | tf_op jit(solution)/shard_map/members/pallas_call | solution.py:113
  31.7 7.0 %base.3 = (f32[4,8,64,128]{3,2,1,0:T(8,128)}, f32[8,128]{1,0:T(8,128)}) custom-call(s32[18]{0:T(128)} %get-tuple-element.25.meta, f32[4,4]{1,0:T(4,128)} %coupling.3, f32[2,32,128]{2,1,0:T(8,128)} %get-tuple-element.30.rows, f32[2,32,64]{2,1,0:T(8,128)} %get-tuple-element.31.cols, f32[4,8,64,128]{3,2,1,0:T(8,128)} %state.1, f32[4,8,64,128]{3,2,1,0:T(8,128)} %old.1), custom_call_target="tpu_custom_call" | custom-call | tf_op jit(solution)/shard_map/base/pallas_call | solution.py:576
  38.7 13.2 %fine.1 = (f32[4,8,66,1,264]{4,3,2,1,0:T(1,128)}, f32[4,176,128]{2,1,0:T(8,128)}, f32[8,128]{1,0:T(8,128)}) custom-call(s32[18]{0:T(128)} %get-tuple-element.25.meta, f32[4,4]{1,0:T(4,128)} %coupling.3, f32[4,128,128]{2,1,0:T(8,128)} %members.1.gath, f32[2,32,264]{2,1,0:T(8,128)} %get-tuple-element.34.halo, f32[8,128]{1,0:T(8,128)} %get-tuple-element.35.sums, ...), custom_call_target="tpu_custom_call" | custom-call | tf_op jit(solution)/shard_map/fine/pallas_call | solution.py:598
  51.8 44.7 %owners.3 = (f32[8,4,176,128]{3,2,1,0:T(8,128)}, f32[8,8,128]{2,1,0:T(8,128)}) custom-call(f32[4,176,128]{2,1,0:T(8,128)} %get-tuple-element.36.refs_0_, f32[8,128]{1,0:T(8,128)} %get-tuple-element.37.refs_1_), custom_call_target="tpu_custom_call" | custom-call | tf_op jit(solution)/shard_map/owners/pallas_call | solution.py:113
  96.5 3.3 %sort.1 = (f32[4,4,176,128]{3,2,1,0:T(8,128)}, f32[8,128]{1,0:T(8,128)}) custom-call(s32[18]{0:T(128)} %get-tuple-element.25.meta, f32[8,4,176,128]{3,2,1,0:T(8,128)} %get-tuple-element.38.got, f32[8,8,128]{2,1,0:T(8,128)} %get-tuple-element.39.sums), custom_call_target="tpu_custom_call" | custom-call | tf_op jit(solution)/shard_map/sort/pallas_call | solution.py:630
  99.8 21.3 %columns.1 = (f32[4,4,176,128]{3,2,1,0:T(8,128)}, f32[4,8,128]{2,1,0:T(8,128)}) custom-call(f32[4,4,176,128]{3,2,1,0:T(8,128)} %get-tuple-element.40.refs_0_, f32[8,128]{1,0:T(8,128)} %get-tuple-element.41.refs_1_), custom_call_target="tpu_custom_call" | custom-call | tf_op jit(solution)/shard_map/columns/pallas_call | solution.py:113
  121.2 3.7 %place.1 = (f32[4,8,64,128]{3,2,1,0:T(8,128)}, f32[1,1]{1,0:T(1,128)}) custom-call(s32[18]{0:T(128)} %get-tuple-element.25.meta, f32[4,8,64,128]{3,2,1,0:T(8,128)} %get-tuple-element.32.tend, f32[4,4,176,128]{3,2,1,0:T(8,128)} %get-tuple-element.42.got, f32[4,8,128]{2,1,0:T(8,128)} %get-tuple-element.43.sums), custom_call_target="tpu_custom_call" | custom-call | tf_op jit(solution)/shard_map/place/pallas_call | solution.py:641
